TPU v7x, 8 devices: a whole 2x2x1 slice. The times are simulated.
8 devices in a mesh: dp: 2 (over z, y), ep: 4 (over x, core).
Axes of the slice: x: 2, y: 2, z: 1, core: 2. Of those that a mesh axis runs over, the one named last changes fastest.
Arguments:
- x_rows: bfloat16 [4096, 2048], P(('dp', 'ep')), parts along dimension 0
- sel_idx: int32 [128, 32], P(('dp', 'ep')), parts along dimension 0
- gate_w: float32 [128, 32], P(('dp', 'ep')), parts along dimension 0
- w_up: bfloat16 [64, 2048, 1024], P('ep')
- w_down: bfloat16 [64, 1024, 2048], P('ep')
Outputs:
- output: bfloat16 [4096, 2048], P(('dp', 'ep')), parts along dimension 0
There are 2 independent parts. A program takes and returns all parts, laid end to end along the dimension named above; an argument that names none is the same for every part.
All inputs are finite; a program needn't handle non-finite values.
Results may differ from a plain program's by a relative error of at most 0.001.
Values are sent between devices in bfloat16 or wider.
A program may use at most 1 GiB of HBM per device.

v0:
```python
import jax
import jax.numpy as jnp
from jax import lax
from jax.sharding import PartitionSpec as P


def solution(mesh):
    group_size = mesh.shape["ep"]

    def local_layer(x_loc, sel_loc, gate_loc, up_loc, down_loc):
        tok_loc, model_width = x_loc.shape
        exp_loc, cap_rows = sel_loc.shape
        entry_count = exp_loc * cap_rows
        pair_cap = 2 * entry_count // group_size
        flat_sel = sel_loc.reshape(entry_count)
        src_dev = flat_sel // tok_loc
        local_row = flat_sel - src_dev * tok_loc
        sort_order = jnp.argsort(src_dev, stable=True)
        position = jnp.argsort(sort_order)
        counts = jnp.bincount(src_dev, length=group_size)
        starts = jnp.cumsum(counts) - counts
        slot_idx = src_dev * pair_cap + position - starts[src_dev]
        request = jnp.zeros((group_size * pair_cap,), jnp.int32).at[slot_idx].set(local_row, unique_indices=True)
        wanted = lax.all_to_all(request.reshape(group_size, pair_cap), "ep", 0, 0, tiled=True).reshape(group_size * pair_cap)
        send_rows = jnp.take(x_loc, wanted, axis=0).reshape(group_size, pair_cap, model_width)
        received = lax.all_to_all(send_rows, "ep", 0, 0, tiled=True).reshape(group_size * pair_cap, model_width)
        picked = jnp.take(received, slot_idx, axis=0).reshape(exp_loc, cap_rows, model_width)
        hidden = jax.nn.gelu(jnp.einsum("ecd,edf->ecf", picked, up_loc, preferred_element_type=jnp.float32), approximate=True).astype(jnp.bfloat16)
        out_rows = jnp.einsum("ecf,efd->ecd", hidden, down_loc, preferred_element_type=jnp.float32)
        contrib = (out_rows * gate_loc[:, :, None]).astype(jnp.bfloat16).reshape(entry_count, model_width)
        back_rows = jnp.zeros((group_size * pair_cap, model_width), jnp.bfloat16).at[slot_idx].set(contrib, unique_indices=True)
        returned = lax.all_to_all(back_rows.reshape(group_size, pair_cap, model_width), "ep", 0, 0, tiled=True).reshape(group_size * pair_cap, model_width)
        summed = jax.ops.segment_sum(returned.astype(jnp.float32), wanted, num_segments=tok_loc)
        return (x_loc.astype(jnp.float32) + summed).astype(jnp.bfloat16)

    row_spec = P(("dp", "ep"), None)
    weight_spec = P("ep", None, None)
    return jax.shard_map(local_layer, mesh=mesh, in_specs=(row_spec, row_spec, row_spec, weight_spec, weight_spec), out_specs=row_spec, check_vma=False)
```

profile of v0, /device:TPU:0, one launch (start us, length us, event | category | flops | bytes accessed | tf_op | source)
XLA Modules:
  0.0 232.1 jit_solution(10733156906886517497)
XLA Ops:
  0.0 0.8 reshape.202
  0.8 0.8 reshape.203
  1.6 4.1 %scatter_custom_fusion = s32[4]{0:T(128)S(1)} fusion(s32[512]{0:T(512)S(1)} %bitcast.42, s32[512]{0:T(512)S(1)} %ne.44, s32[]{:T(128)} %constant.26.clone.1), kind=kCustom, calls=%fused_computation.52 | custom fusion | flops 512 | bytes 20 | tf_op jit(solution)/shard_map/scatter-add | solution.py:20
  5.7 0.2 reduce-window.9
  5.9 0.7 fusion.32
  6.5 3.8 %sort.34 = (s32[512]{0:T(512)}, s32[512]{0:T(512)S(1)}) sort(s32[512]{0:T(512)S(1)} %get-tuple-element.14, s32[512]{0:T(512)S(1)} %iota.8), dimensions={0}, to_apply=%region_0.1 | sort | flops 4608 | bytes 8192 | tf_op jit(solution)/shard_map/jit(argsort)/sort | solution.py:18
  10.3 3.8 %sort.35 = (s32[512]{0:T(512)}, s32[512]{0:T(512)S(1)}) sort(s32[512]{0:T(512)S(1)} %get-tuple-element.7, s32[512]{0:T(512)S(1)} %iota.9), dimensions={0}, to_apply=%region_1.2 | sort | flops 4608 | bytes 8192 | tf_op jit(solution)/shard_map/jit(argsort)/sort | solution.py:19
  14.1 2.5 %compare_select_fusion.3 = s32[512,1]{0,1:T(1,128)S(1)} fusion(s32[512,1]{0,1:T(1,128)S(1)} %get-tuple-element.12, s32[]{:T(128)} %bitcast.3, s32[]{:T(128)} %bitcast.4, s32[]{:T(128)} %bitcast.6, s32[]{:T(128)} %bitcast.5), kind=kLoop, calls=%fused_computation.28 | loop fusion | flops 4608 | bytes 4112 | tf_op jit(solution)/shard_map/gather | solution.py:22
  16.6 2.4 %scatter_custom_fusion.1 = s32[1024]{0:T(1024)S(1)} fusion(s32[512]{0:T(512)S(1)} %get-tuple-element.10, s32[512]{0:T(512)S(1)} %get-tuple-element.13, s32[]{:T(128)} %constant.26.clone.1), kind=kCustom, calls=%fused_computation.46 | custom fusion | bytes 4100 | tf_op jit(solution)/shard_map/scatter | solution.py:23
  19.1 8.2 %all_to_all.19 = s32[4,1,256]{2,1,0:T(1,128)S(1)} all-to-all(s32[4,1,256]{2,1,0:T(1,128)S(1)} %bitcast.39), channel_id=1, replica_groups=mesh['dp'=2,'ep'=4] {'ep'}, dimensions={0} | all-to-all | bytes 8192 | tf_op jit(solution)/shard_map/all_to_all | solution.py:24
  27.3 10.7 %gather_fusion = bf16[1024,2048]{1,0:T(8,128)(2,1)} fusion(bf16[512,2048]{1,0:T(8,128)(2,1)} %param.5, s32[1024]{0:T(1024)S(1)} %broadcast_clamp_fusion), kind=kCustom, calls=%fused_computation | custom fusion | bytes 8392704 | tf_op jit(solution)/shard_map/jit(_take)/gather | solution.py:25
  38.0 4.6 %broadcast_select_fusion = bf16[4,256,2048]{2,1,0:T(8,128)(2,1)} fusion(bf16[4,256,2048]{2,1,0:T(8,128)(2,1)} %bitcast.33, pred[4,256]{1,0:T(4,128)(4,1)S(1)} %compare_and_fusion), kind=kLoop, calls=%fused_computation.9 | loop fusion | flops 2097152 | bytes 8389632 | tf_op jit(solution)/shard_map/jit(_take)/select_n | solution.py:25
  42.6 5.0 %all-to-all-start.1 = ((bf16[4,256,2048]{2,1,0:T(8,128)(2,1)}), bf16[4,256,2048]{2,1,0:T(8,128)(2,1)}, u32[]{:S(2)}, u32[]{:S(2)}) async-start(bf16[4,256,2048]{2,1,0:T(8,128)(2,1)} %broadcast_select_fusion), calls=%async_computation.1 | async-start | bytes 8388608 | tf_op jit(solution)/shard_map/all_to_all | solution.py:26
  47.6 0.1 broadcast_in_dim.44
  47.7 47.6 %all-to-all-done.1 = bf16[4,256,2048]{2,1,0:T(8,128)(2,1)} async-done(((bf16[4,256,2048]{2,1,0:T(8,128)(2,1)}), bf16[4,256,2048]{2,1,0:T(8,128)(2,1)}, u32[]{:S(2)}, u32[]{:S(2)}) %all-to-all-start.1) | async-done | bytes 4194336 | tf_op jit(solution)/shard_map/all_to_all | solution.py:26
  95.3 7.1 %gather_fusion.1 = bf16[512,2048]{1,0:T(8,128)(2,1)S(1)} fusion(bf16[1024,2048]{1,0:T(8,128)(2,1)} %bitcast.13, s32[1024]{0:T(1024)S(1)} %pad_clamp_fusion), kind=kCustom, calls=%fused_computation.1 | custom fusion | bytes 4196352 | tf_op jit(solution)/shard_map/jit(_take)/gather | solution.py:27
  102.4 0.0 copy-start.1
  102.5 24.1 %fusion.9.clone.4 = bf16[16,32,1024]{2,1,0:T(8,128)(2,1)S(1)} fusion(bf16[16,2048,1024]{2,1,0:T(8,128)(2,1)} %param.8, bf16[16,32,2048]{2,1,0:T(8,128)(2,1)S(1)} %bitcast.35, pred[16,32]{1,0:T(8,128)(4,1)S(1)} %broadcast_in_dim.44), kind=kOutput, calls=%fused_computation.18.clone.clone.clone.1 | convolution fusion | flops 2153250816 | bytes 70255104 | tf_op jit(solution)/shard_map/ecd,edf->ecf/dot_general | solution.py:28
  126.6 0.0 copy-done.1
  126.6 23.6 %multiply_convert_fusion = bf16[16,32,2048]{2,1,0:T(8,128)(2,1)S(1)} fusion(bf16[16,1024,2048]{2,1,0:T(8,128)(2,1)} %param.9, f32[16,32]{1,0:T(8,128)S(1)} %copy-done.1, bf16[16,32,1024]{2,1,0:T(8,128)(2,1)S(1)} %fusion.9.clone.4), kind=kOutput, calls=%fused_computation.8 | convolution fusion | flops 2149580800 | bytes 70256640 | tf_op jit(solution)/shard_map/ecf,efd->ecd/dot_general | solution.py:29
  150.2 6.4 %scatter_custom_fusion.2 = bf16[1024,2048]{1,0:T(8,128)(2,1)} fusion(s32[512]{0:T(512)S(1)} %get-tuple-element.10, bf16[512,2048]{1,0:T(8,128)(2,1)S(1)} %bitcast.36, bf16[]{:T(256)} %constant.63.clone.1), kind=kCustom, calls=%fused_computation.21 | custom fusion | bytes 4194306 | tf_op jit(solution)/shard_map/scatter | solution.py:31
  156.7 0.0 copy-start
  156.7 5.0 %all-to-all-start.2 = ((bf16[4,256,2048]{2,1,0:T(8,128)(2,1)}), bf16[4,256,2048]{2,1,0:T(8,128)(2,1)}, u32[]{:S(2)}, u32[]{:S(2)}) async-start(bf16[4,256,2048]{2,1,0:T(8,128)(2,1)} %bitcast.34), calls=%async_computation.2 | async-start | bytes 8388608 | tf_op jit(solution)/shard_map/all_to_all | solution.py:32
  161.7 0.0 copy-done
  161.7 2.5 %convert_element_type.18 = f32[512,2048]{1,0:T(8,128)} convert(bf16[512,2048]{1,0:T(8,128)(2,1)S(1)} %copy-done) | non-fusion elementwise | flops 1048576 | bytes 6291456 | tf_op jit(solution)/shard_map/convert_element_type | solution.py:34
  164.2 45.4 %all-to-all-done.2 = bf16[4,256,2048]{2,1,0:T(8,128)(2,1)} async-done(((bf16[4,256,2048]{2,1,0:T(8,128)(2,1)}), bf16[4,256,2048]{2,1,0:T(8,128)(2,1)}, u32[]{:S(2)}, u32[]{:S(2)}) %all-to-all-start.2) | async-done | bytes 4194336 | tf_op jit(solution)/shard_map/all_to_all | solution.py:32
  209.5 18.7 %scatter_custom_fusion.3 = f32[512,2048]{1,0:T(8,128)} fusion(f32[512,2048]{1,0:T(8,128)} %convert_element_type.18, s32[1024]{0:T(1024)S(1)} %bitcast.38, bf16[1024,2048]{1,0:T(8,128)(2,1)} %bitcast.18), kind=kCustom, calls=%fused_computation.6 | custom fusion | flops 4194304 | bytes 8388608 | tf_op jit(solution)/shard_map/scatter-add | solution.py:33
  228.3 3.8 %convert_element_type.23 = bf16[512,2048]{1,0:T(8,128)(2,1)} convert(f32[512,2048]{1,0:T(8,128)} %scatter_custom_fusion.3) | non-fusion elementwise | flops 1048576 | bytes 6291456 | tf_op jit(solution)/shard_map/convert_element_type | solution.py:34
  (11 shorter events, 0.1 us)
Async XLA Ops:
  42.6 52.7 %all-to-all-start.1 = ((bf16[4,256,2048]{2,1,0:T(8,128)(2,1)}), bf16[4,256,2048]{2,1,0:T(8,128)(2,1)}, u32[]{:S(2)}, u32[]{:S(2)}) async-start(bf16[4,256,2048]{2,1,0:T(8,128)(2,1)} %broadcast_select_fusion), calls=%async_computation.1 | async-start | bytes 8388608 | tf_op jit(solution)/shard_map/all_to_all | solution.py:26
  102.4 24.1 %copy-start.1 = (f32[16,32]{1,0:T(8,128)S(1)}, f32[16,32]{1,0:T(8,128)}, u32[]{:S(2)}) copy-start(f32[16,32]{1,0:T(8,128)} %param.7) | copy-start | bytes 6148
  156.7 5.0 %copy-start = (bf16[512,2048]{1,0:T(8,128)(2,1)S(1)}, bf16[512,2048]{1,0:T(8,128)(2,1)}, u32[]{:S(2)}) copy-start(bf16[512,2048]{1,0:T(8,128)(2,1)} %param.5) | copy-start | bytes 6291460
  156.7 52.9 %all-to-all-start.2 = ((bf16[4,256,2048]{2,1,0:T(8,128)(2,1)}), bf16[4,256,2048]{2,1,0:T(8,128)(2,1)}, u32[]{:S(2)}, u32[]{:S(2)}) async-start(bf16[4,256,2048]{2,1,0:T(8,128)(2,1)} %bitcast.34), calls=%async_computation.2 | async-start | bytes 8388608 | tf_op jit(solution)/shard_map/all_to_all | solution.py:32
where the time goes:
time: 233 us; the launch traced here: 232 us
  waiting for transfers between devices  93 us (40%)
  matrix products  47.7 us (20%)
  other arithmetic  44 us (19%)
  local copies, waits for them, and re-layouts  29 us (12%)
  starting transfers between devices  10 us (4%)
  blocking collectives  8.21 us (4%)
    all_to_all x1, waiting for transfers between devices, local_layer(): lax.all_to_all(send_rows, 'ep', 0, 0, tiled=True)  47.6 us
    all_to_all x1, waiting for transfers between devices, local_layer(): lax.all_to_all(back_rows.reshape(group_size, pair_cap, model_width), 'ep'...  45.4 us
    dot_general x1, matrix products, local_layer(): jnp.einsum('ecd,edf->ecf', picked, up_loc, preferred_element_type=jnp.flo...  24.1 us
    dot_general x1, matrix products, local_layer(): jnp.einsum('ecf,efd->ecd', hidden, down_loc, preferred_element_type=jnp.f...  23.6 us
    scatter-add x1, other arithmetic, local_layer(): jax.ops.segment_sum(returned.astype(jnp.float32), wanted, num_segments=to...  18.7 us
    gather x1, local copies, waits for them, and re-layouts, local_layer(): jnp.take(x_loc, wanted, axis=0).reshape(group_size, pair_cap, model_width)  10.7 us
    all_to_all x1, blocking collectives, local_layer(): lax.all_to_all(request.reshape(group_size, pair_cap), 'ep', 0, 0, tiled=T...  8.21 us
    gather x1, local copies, waits for them, and re-layouts, local_layer(): jnp.take(received, slot_idx, axis=0).reshape(exp_loc, cap_rows, model_width)  7.13 us
  transfers between devices with their start and end apart: 2, of which 2 were waited for; matrix products, arithmetic and copies ran while one was open for 1% of the time, Pallas kernels for 0%

commit v1 on v0

v1 whole, which is shorter than its diff:
```python
import functools

import jax
import jax.numpy as jnp
from jax import lax
from jax.experimental import pallas as pl
from jax.experimental.pallas import tpu as pltpu
from jax.sharding import PartitionSpec as P

MESH = pl.DeviceIdType.MESH
CHUNKS = 4
RING = 3


def moe_kernel(sel_col, slot_of, gate_of, tab, x_hbm, up_hbm, down_hbm, y_ref,
               x_all, picked, hot, acc, outbox, inbox, tabs, up_buf, down_buf,
               x_sem, up_sem, down_sem, send_link, recv_link, send_fwd, recv_fwd, send_near, recv_near,
               send_tab, recv_tab, send_ret, recv_ret):
    tok, width = y_ref.shape
    experts = slot_of.shape[0]
    cap = slot_of.shape[1]
    part = cap // 2
    half = experts // 2
    rows = tok // CHUNKS
    me = lax.axis_index("ep")
    near = me + 1 - 2 * (me % 2)
    far = (me + 2) % 4
    diag = 3 - me
    peers = (near, far, diag)
    chip = me // 2
    own = pl.multiple_of(me * tok, tok)

    def up_copy(e):
        return pltpu.make_async_copy(up_hbm.at[e], up_buf.at[e % RING], up_sem.at[e % RING])

    def down_copy(e):
        return pltpu.make_async_copy(down_hbm.at[e], down_buf.at[e % RING], down_sem.at[e % RING])

    def remote(src, dst, send, recv, peer):
        return pltpu.make_async_remote_copy(src_ref=src, dst_ref=dst, send_sem=send, recv_sem=recv,
                                            device_id={"ep": peer}, device_id_type=MESH)

    load_x = pltpu.make_async_copy(x_hbm, x_all.at[pl.ds(own, tok)], x_sem)
    load_x.start()
    for e in range(RING):
        up_copy(e).start()
        down_copy(e).start()

    barrier = pltpu.get_barrier_semaphore()
    for peer in peers:
        pl.semaphore_signal(barrier, inc=1, device_id={"ep": peer}, device_id_type=MESH)
    pl.semaphore_wait(barrier, 3)

    def chunk_at(dev, c):
        return x_all.at[pl.ds(pl.multiple_of(dev * tok + c * rows, rows), rows)]

    load_x.wait()
    link = [remote(chunk_at(me, c), chunk_at(me, c), send_link.at[c], recv_link.at[c], far) for c in range(CHUNKS)]
    for copy in link:
        copy.start()
    whole = x_all.at[pl.ds(own, tok)]
    to_near = remote(whole, whole, send_near, recv_near, near)
    to_near.start()
    table = [remote(tab.at[peer], tabs.at[me], send_tab.at[i], recv_tab.at[i], peer) for i, peer in enumerate(peers)]
    for copy in table:
        copy.start()
    tabs[me] = tab[me]
    acc[...] = x_all[pl.ds(own, tok), :].astype(jnp.float32)

    def pick(start, size, first):
        col = lax.broadcasted_iota(jnp.int32, (experts * cap, size), 1) + start
        hot[:, 0:size] = jnp.where(sel_col[...] == col, 1.0, 0.0).astype(jnp.bfloat16)

        @pl.loop(0, width // 256)
        def _(n):
            cols = pl.ds(pl.multiple_of(n * 256, 256), 256)
            got = jnp.dot(hot[:, 0:size], x_all[pl.ds(pl.multiple_of(start, size), size), cols],
                          preferred_element_type=jnp.float32).astype(jnp.bfloat16)
            if first:
                picked[:, cols] = got
            else:
                picked[:, cols] = picked[:, cols] + got

    pick(own, tok, True)
    to_near.wait()
    pick(near * tok, tok, False)
    forward = [remote(chunk_at(far, c), chunk_at(far, c), send_fwd.at[c], recv_fwd.at[c], near) for c in range(CHUNKS)]
    for c in range(CHUNKS):
        link[c].wait_recv()
        forward[c].start()
        pick(far * tok + c * rows, rows, False)
        forward[c].wait_recv()
        pick(diag * tok + c * rows, rows, False)

    def one_hot_t(h, pair):
        idx = jnp.concatenate([tabs[pair * 2, h], tabs[pair * 2 + 1, h]], axis=1)
        row = lax.broadcasted_iota(jnp.int32, (tok, idx.shape[1]), 0)
        hot[:, 0:idx.shape[1]] = jnp.where(row == idx, 1.0, 0.0).astype(jnp.bfloat16)

    def add_pair(h, pair):
        one_hot_t(h, pair)
        depth = 2 * half * part

        @pl.loop(0, width // 256)
        def _(n):
            cols = pl.ds(pl.multiple_of(n * 256, 256), 256)
            acc[:, cols] += jnp.dot(hot[:, 0:depth], inbox[h, pl.ds(pair * depth, depth), cols],
                                    preferred_element_type=jnp.float32)

    def from_peer(i, h):
        block = inbox.at[h, pl.ds(pl.multiple_of(peers[i] * half * part, half * part), half * part)]
        return remote(block, block, send_ret.at[i, h], recv_ret.at[i, h], peers[i])

    def expert(e, carry):
        h = e // half
        up_copy(e).wait()
        z = jnp.dot(picked[pl.ds(pl.multiple_of(e * cap, cap), cap), :], up_buf[e % RING],
                    preferred_element_type=jnp.float32)
        act = (0.5 * z * (1.0 + jnp.tanh(0.7978845608028654 * (z + 0.044715 * (z * z * z))))).astype(jnp.bfloat16)

        @pl.when(e + RING < experts)
        def _():
            up_copy(e + RING).start()

        place = slot_of[pl.ds(e, 1), :] == lax.broadcasted_iota(jnp.int32, (4 * part, cap), 0)
        perm = jnp.where(place, 1.0, 0.0)
        gate = jnp.sum(perm * gate_of[pl.ds(e, 1), :], axis=1, keepdims=True)
        act = jnp.dot(perm.astype(jnp.bfloat16), act, preferred_element_type=jnp.float32).astype(jnp.bfloat16)
        down_copy(e).wait()
        for n in range(width // 512):
            cols = slice(n * 512, (n + 1) * 512)
            o = jnp.dot(act, down_buf[e % RING, :, cols], preferred_element_type=jnp.float32)
            outbox[e, :, cols] = (o * gate).astype(jnp.bfloat16)

        @pl.when(e + RING < experts)
        def _():
            down_copy(e + RING).start()

        spot = pl.ds(pl.multiple_of(me * half * part + (e % half) * part, part), part)
        for i in (1, 2, 0):
            remote(outbox.at[e, pl.ds(pl.multiple_of(peers[i] * part, part), part)], inbox.at[h, spot],
                   send_ret.at[i, h], recv_ret.at[i, h], peers[i]).start()
        inbox[h, spot, :] = outbox[e, pl.ds(pl.multiple_of(me * part, part), part), :]

        @pl.when(e == experts - 3)
        def _():
            for copy in table:
                copy.wait()
            for i in range(3):
                from_peer(i, 0).wait_recv()
            add_pair(0, 0)
            add_pair(0, 1)
        return carry

    lax.fori_loop(0, experts, expert, 0)
    from_peer(0, 1).wait_recv()
    add_pair(1, chip)
    from_peer(1, 1).wait_recv()
    from_peer(2, 1).wait_recv()
    add_pair(1, 1 - chip)
    y_ref[...] = acc[...].astype(jnp.bfloat16)

    for c in range(CHUNKS):
        link[c].wait_send()
        forward[c].wait_send()
    for h in range(2):
        for i in range(3):
            from_peer(i, h).wait_send()


def solution(mesh):
    group_size = mesh.shape["ep"]

    def local_layer(x_loc, sel_loc, gate_loc, up_loc, down_loc):
        tok, width = x_loc.shape
        experts, cap = sel_loc.shape
        hidden = up_loc.shape[2]
        part = cap // 2
        owner = sel_loc // tok
        local_row = sel_loc - owner * tok
        same = owner[:, :, None] == owner[:, None, :]
        before = jnp.arange(cap)[None, :, None] > jnp.arange(cap)[None, None, :]
        rank = jnp.sum((same & before).astype(jnp.int32), axis=2)
        slot = owner * part + rank
        hit = slot[:, None, :] == jnp.arange(group_size * part)[None, :, None]
        tab = jnp.max(jnp.where(hit, local_row[:, None, :], -1), axis=2)
        tab = tab.reshape(experts, group_size, part).transpose(1, 0, 2).reshape(group_size, 2, 1, experts * part // 2)
        sel_col = sel_loc.reshape(experts * cap, 1)
        vmem = pl.BlockSpec(memory_space=pltpu.VMEM)
        hbm = pl.BlockSpec(memory_space=pl.ANY)
        bf16 = jnp.bfloat16
        dma = pltpu.SemaphoreType.DMA
        return pl.pallas_call(
            moe_kernel,
            out_shape=jax.ShapeDtypeStruct((tok, width), bf16),
            in_specs=[vmem, vmem, vmem, vmem, hbm, hbm, hbm],
            out_specs=vmem,
            scratch_shapes=[
                pltpu.VMEM((group_size * tok, width), bf16),
                pltpu.VMEM((experts * cap, width), bf16),
                pltpu.VMEM((tok, tok), bf16),
                pltpu.VMEM((tok, width), jnp.float32),
                pltpu.VMEM((experts, group_size * part, width), bf16),
                pltpu.VMEM((2, group_size * experts * part // 2, width), bf16),
                pltpu.VMEM(tab.shape, jnp.int32),
                pltpu.VMEM((RING, width, hidden), bf16),
                pltpu.VMEM((RING, hidden, width), bf16),
                dma, dma((RING,)), dma((RING,)),
                dma((CHUNKS,)), dma((CHUNKS,)), dma((CHUNKS,)), dma((CHUNKS,)), dma, dma,
                dma((3,)), dma((3,)), dma((3, 2)), dma((3, 2)),
            ],
            compiler_params=pltpu.CompilerParams(collective_id=0, has_side_effects=True,
                                                 vmem_limit_bytes=64 * 1024 * 1024 - 65536),
        )(sel_col, slot, gate_loc, tab, x_loc, up_loc, down_loc)

    row_spec = P(("dp", "ep"), None)
    weight_spec = P("ep", None, None)
    return jax.shard_map(local_layer, mesh=mesh, in_specs=(row_spec, row_spec, row_spec, weight_spec, weight_spec), out_specs=row_spec, check_vma=False)
```

time: 233 us -> 119 us (0.51)
  Pallas kernels: 0 us -> 111 us
  waiting for transfers between devices: 93 us -> 0 us
  matrix products: 47.7 us -> 0 us
  other arithmetic: 44 us -> 2.1 us
  local copies, waits for them, and re-layouts: 29 us -> 6.17 us
  starting transfers between devices: 10 us -> 0 us
  blocking collectives: 8.21 us -> 0 us
    pallas_call x0 -> x1, Pallas kernels: none -> 111 us  [local_layer(): pl.pallas_call(moe_kernel, out_shape=jax.ShapeDtypeStruct((tok, width), b...]
    all_to_all x2 -> x0, waiting for transfers between devices: 93 us -> none  [the longest x1 47.6 us: local_layer(): lax.all_to_all(send_rows, 'ep', 0, 0, tiled=True)]
    dot_general x2 -> x0, matrix products: 47.7 us -> none  [the longest x1 24.1 us: local_layer(): jnp.einsum('ecd,edf->ecf', picked, up_loc, preferred_element_type=jnp.flo...]
    scatter-add x2 -> x0, other arithmetic: 22.8 us -> none  [the longest x1 18.7 us: local_layer(): jax.ops.segment_sum(returned.astype(jnp.float32), wanted, num_segments=to...]
    gather x3 -> x0, local copies, waits for them, and re-layouts: 18.5 us -> none  [the longest x1 10.7 us: local_layer(): jnp.take(x_loc, wanted, axis=0).reshape(group_size, pair_cap, model_width)]
    all_to_all x2 -> x0, starting transfers between devices: 10 us -> none  [the longest x1 5.02 us: local_layer(): lax.all_to_all(send_rows, 'ep', 0, 0, tiled=True)]
    scatter x2 -> x0, local copies, waits for them, and re-layouts: 8.89 us -> none  [the longest x1 6.45 us: local_layer(): jnp.zeros((group_size * pair_cap, model_width), jnp.bfloat16).at[slot_idx]]
    all_to_all x1 -> x0, blocking collectives: 8.21 us -> none  [local_layer(): lax.all_to_all(request.reshape(group_size, pair_cap), 'ep', 0, 0, tiled=T...]
  transfers between devices with their start and end apart: 2 -> 0, of which waited for: 2 -> 0; matrix products, arithmetic and copies ran while one was open for 1% -> 0% of each run, Pallas kernels for 0% -> 0%
where the time goes in v1:
time: 119 us
  Pallas kernels  111 us (93%)
  local copies, waits for them, and re-layouts  6.17 us (5%)
  other arithmetic  2.1 us (2%)
    pallas_call x1, Pallas kernels, local_layer(): pl.pallas_call(moe_kernel, out_shape=jax.ShapeDtypeStruct((tok, width), b...  111 us
    unnamed x3, local copies, waits for them, and re-layouts  3.75 us

profile of v1, /device:TPU:0, one launch (start us, length us, event | category | flops | bytes accessed | tf_op | source)
XLA Modules:
  0.0 118.9 jit_solution(2377013486343946799)
XLA Ops:
  0.0 0.7 add_select_fusion
  0.7 0.5 convert_reduce_fusion
  1.2 0.7 multiply_subtract_fusion
  1.9 0.0 copy-start
  1.9 0.6 copy-done
  2.5 0.2 select_reduce_fusion
  2.7 0.1 reshape.29
  2.8 0.7 reshape.30.tab
  3.5 1.7 %reshape.31.sel_col = s32[512,1]{1,0:T(8,128)} reshape(s32[16,32]{1,0:T(8,128)} %param.6) | data formatting | bytes 4096 | tf_op jit(solution)/shard_map/reshape | solution.py:188
  5.1 110.6 %shard_map.55 = bf16[512,2048]{1,0:T(8,128)(2,1)} custom-call(s32[512,1]{1,0:T(8,128)} %reshape.31.sel_col, s32[16,32]{1,0:T(8,128)} %copy-done, f32[16,32]{1,0:T(8,128)} %gate_of.1, s32[4,2,1,128]{3,2,1,0:T(1,128)} %reshape.30.tab, bf16[512,2048]{1,0:T(8,128)(2,1)} %x_hbm.1, bf16[16,2048,1024]{2,1,0:T(8,128)(2,1)} %up_hbm.1, bf16[16,1024,2048]{2,1,0:T(8,128)(2,1)} %down_hbm.1), custom_call_target="tpu_custom_call" | custom-call | tf_op jit(solution)/shard_map/pallas_call | solution.py:193
  115.7 3.2 %copy.11 = bf16[512,2048]{1,0:T(8,128)(2,1)} copy(bf16[512,2048]{1,0:T(8,128)(2,1)} %shard_map.55) | data formatting | bytes 4194304
  (2 shorter events, 0.0 us)
Async XLA Ops:
  1.9 0.6 copy-start

commit v2 on v0

v2 whole, which is shorter than its diff:
```python
import functools

import jax
import jax.numpy as jnp
from jax import lax
from jax.experimental import pallas as pl
from jax.experimental.pallas import tpu as pltpu
from jax.sharding import PartitionSpec as P

MESH = pl.DeviceIdType.MESH
RING = 3
GROUPS = 4
LANES = 128
BF16 = jnp.bfloat16
F32 = jnp.float32
I32 = jnp.int32


def iota(shape, dim):
    return lax.broadcasted_iota(I32, shape, dim)


def mm(a, b):
    return jnp.dot(a.astype(BF16), b.astype(BF16), preferred_element_type=F32)


def mm_t(a, b):
    return lax.dot_general(a.astype(BF16), b.astype(BF16), (((1,), (1,)), ((), ())), preferred_element_type=F32)


def flag(cond):
    return jnp.where(cond, 1.0, 0.0)


def total(a):
    return jnp.sum(jnp.sum(a, axis=1, keepdims=True), axis=0, keepdims=True)


def moe_kernel(xcap, rcap, checked, sel_in, gate_in, x_hbm, up_hbm, down_hbm, y_ref, ok_ref,
               x_chip, x_out, x_in, picked, contrib, contrib_near, ret_out, ret_in, acc, hot,
               sels, slots, toks, sel_col, gate_col, need_col, pos_out, square, ok_mine, ok_other, up_buf, down_buf,
               x_sem, up_sem, down_sem, send_sel, recv_sel, send_x, recv_x, send_link, recv_link, send_fwd, recv_fwd,
               send_near, recv_near, send_ret, recv_ret, send_back, recv_back, send_ok, recv_ok):
    tok, width = y_ref.shape
    cap = 32
    experts = GROUPS * LANES // cap
    per_group = experts // GROUPS
    xoff = [sum(xcap[:i]) for i in range(GROUPS + 1)]
    roff = [sum(rcap[:i]) for i in range(GROUPS + 1)]
    me = lax.axis_index("ep")
    core = me % 2
    chip = me // 2
    near = me + 1 - 2 * core
    far = (me + 2) % 4
    diag = 3 - me
    peers = (near, far, diag)
    other_group = 1 - lax.axis_index("dp")

    def up_copy(e):
        return pltpu.make_async_copy(up_hbm.at[e], up_buf.at[e % RING], up_sem.at[e % RING])

    def down_copy(e):
        return pltpu.make_async_copy(down_hbm.at[e], down_buf.at[e % RING], down_sem.at[e % RING])

    def remote(src, dst, send, recv, peer, axis="ep"):
        return pltpu.make_async_remote_copy(src_ref=src, dst_ref=dst, send_sem=send, recv_sem=recv,
                                            device_id={axis: peer}, device_id_type=MESH)

    own_rows = pl.ds(pl.multiple_of(core * tok, tok), tok)
    near_rows = pl.ds(pl.multiple_of((1 - core) * tok, tok), tok)
    load_x = pltpu.make_async_copy(x_hbm, x_chip.at[own_rows], x_sem)
    load_x.start()

    barrier = pltpu.get_barrier_semaphore()
    for peer in peers:
        pl.semaphore_signal(barrier, inc=1, device_id={"ep": peer}, device_id_type=MESH)
    if checked:
        pl.semaphore_signal(barrier, inc=1, device_id={"dp": other_group}, device_id_type=MESH)
    for e in range(RING):
        up_copy(e).start()
        down_copy(e).start()
    pl.semaphore_wait(barrier, 4 if checked else 3)

    sel_send = [remote(sel_in, sels.at[me], send_sel.at[i], recv_sel.at[i], peer) for i, peer in enumerate(peers)]
    for copy in sel_send:
        copy.start()
    load_x.wait()
    to_near = remote(x_chip.at[own_rows], x_chip.at[own_rows], send_x, recv_x, near)
    to_near.start()
    sels[me] = sel_in[...]

    square[...] = jnp.zeros_like(square)
    square[0:GROUPS, :] = sel_in[...].astype(F32)
    square[8:8 + GROUPS, :] = gate_in[...]
    turned = square[...].T
    for j in range(GROUPS):
        sel_col[j * LANES:(j + 1) * LANES, :] = turned[:, j:j + 1].astype(I32)
        gate_col[j * LANES:(j + 1) * LANES, :] = turned[:, 8 + j:9 + j]
    for copy in sel_send:
        copy.wait_recv()

    before = flag(iota((LANES, LANES), 0) < iota((LANES, LANES), 1))
    ones = jnp.ones((LANES, LANES), F32)
    rows_before = flag(iota((GROUPS * 8, GROUPS * 8), 1) < iota((GROUPS * 8, GROUPS * 8), 0))

    def row_order(c):
        base = (1 - c) * (2 * tok)
        seen = jnp.zeros((8, LANES), F32)
        firsts, fits = [], []
        for j in range(GROUPS):
            row = jnp.concatenate([sels[2 * c, j:j + 1, :], sels[2 * c + 1, j:j + 1, :]], axis=1) - base
            high = flag(iota((8, 2 * LANES), 0) == (row >> 7))
            low = flag(iota((LANES, 2 * LANES), 0) == (row & 127))
            need = flag(mm_t(high, low) > 0.5)
            firsts.append(need * (1.0 - seen))
            seen = jnp.maximum(seen, need)
            fits.append(flag(total(seen) < xoff[j + 1] + 0.5))
        first = jnp.concatenate(firsts, axis=0)
        place = mm(first, before) + mm(rows_before, mm(first, ones))
        pos = sum(firsts[j] * (place[8 * j:8 * j + 8] + 1.0) for j in range(GROUPS)) - 1.0
        return pos, fits[0] * fits[1] * fits[2] * fits[3]

    def entry_order(d):
        away = flag((sels[d] >> 10) != d // 2)
        rank = mm(away, before)
        count = jnp.sum(away, axis=1, keepdims=True)
        end = jnp.zeros((1, 1), F32)
        for j in range(GROUPS):
            begin = jnp.maximum(end, float(roff[j]))
            slots[d, j:j + 1, :] = (away[j:j + 1] * (rank[j:j + 1] + begin + 1.0) - 1.0).astype(I32)
            end = begin + count[j:j + 1]
        return flag(end < roff[GROUPS] + 0.5)

    to_send, fit = row_order(1 - chip)
    pos_out[...] = to_send.astype(I32)
    to_near.wait_recv()

    link = []
    for i in range(GROUPS):
        part = xcap[i] // 2
        start = xoff[i] + core * part
        for b in range(8):
            hot[0:part, b * LANES:(b + 1) * LANES] = flag(iota((part, LANES), 0) + start == pos_out[b:b + 1, :]).astype(BF16)
        at = pl.ds(xoff[i] // 2, part)

        @pl.loop(0, width // 256)
        def _(n):
            cols = pl.ds(pl.multiple_of(n * 256, 256), 256)
            x_out[at, cols] = jnp.dot(hot[0:part, 0:2 * tok], x_chip[:, cols], preferred_element_type=F32).astype(BF16)

        link.append(remote(x_out.at[at], x_in.at[pl.ds(pl.multiple_of(start, 16), part)], send_link.at[i], recv_link.at[i], far))
        link[i].start()

    wanted, fit_in = row_order(chip)
    fit = fit * fit_in
    for d in range(4):
        fit = fit * entry_order(d)

    found = jnp.zeros((GROUPS * LANES, LANES), F32)
    for b in range(8):
        base = (1 - chip) * (2 * tok) + b * LANES
        found = found + jnp.where(sel_col[...] == iota((GROUPS * LANES, LANES), 1) + base, wanted[b:b + 1, :] + 1.0, 0.0)
    need_col[...] = (jnp.sum(found, axis=1, keepdims=True) - 1.0).astype(I32)

    for b in range(8):
        base = chip * (2 * tok) + b * LANES
        hot[:, b * LANES:(b + 1) * LANES] = flag(sel_col[...] == iota((GROUPS * LANES, LANES), 1) + base).astype(BF16)

    @pl.loop(0, width // 256)
    def _(n):
        cols = pl.ds(pl.multiple_of(n * 256, 256), 256)
        picked[:, cols] = jnp.dot(hot[:, 0:2 * tok], x_chip[:, cols], preferred_element_type=F32).astype(BF16)

    for f, d in enumerate((far, diag)):
        row = sels[d]
        for j in range(GROUPS):
            sums = jnp.zeros((8, LANES), F32)
            for k in range(j + 1):
                chosen = flag(iota((LANES, LANES), 0) + roff[j] == slots[d, k:k + 1, :])
                at = iota((8, LANES), 0)
                value = jnp.where(at == 0, row[k:k + 1] >> 5, jnp.where(at == 1, row[k:k + 1] & 31, 1)).astype(F32)
                sums = sums + mm_t(value, chosen)
            token = jnp.where((sums[2:3] > 0.5) & (iota((1, LANES), 1) < rcap[j]), sums[0:1] * 32.0 + sums[1:2], -1.0)
            toks[f, j] = token.astype(I32)

    if checked:
        ok_mine[...] = jnp.broadcast_to(fit, ok_mine.shape)
        ok_send = remote(ok_mine, ok_other, send_ok, recv_ok, other_group, "dp")
        ok_send.start()

    acc[...] = x_chip[own_rows, :].astype(F32)

    forward = []
    for i in range(GROUPS):
        part = xcap[i] // 2
        block = x_in.at[pl.ds(pl.multiple_of(xoff[i] + core * part, 16), part)]
        forward.append(remote(block, block, send_fwd.at[i], recv_fwd.at[i], near))

    def arrive(i):
        link[i].wait_recv()
        forward[i].start()
        r0, size = i * LANES, xcap[i]
        hot[r0:, 0:size] = flag(need_col[r0:, :] == iota((GROUPS * LANES - r0, size), 1) + xoff[i]).astype(BF16)
        forward[i].wait_recv()

        @pl.loop(0, width // 256)
        def _(n):
            cols = pl.ds(pl.multiple_of(n * 256, 256), 256)
            picked[r0:, cols] = picked[r0:, cols] + jnp.dot(
                hot[r0:, 0:size], x_in[xoff[i]:xoff[i + 1], cols], preferred_element_type=F32).astype(BF16)

    pass_near, back = [], []
    for j in range(GROUPS):
        block = pl.ds(j * LANES, LANES)
        pass_near.append(remote(contrib.at[block], contrib_near.at[block], send_near.at[j], recv_near.at[j], near))
        block = pl.ds(roff[j], rcap[j])
        back.append(remote(ret_out.at[block], ret_in.at[0, block], send_ret.at[j], recv_ret.at[j], far))

    def give(j):
        pass_near[j].start()
        depth = (j + 1) * LANES
        for k in range(j + 1):
            hot[0:rcap[j], k * LANES:(k + 1) * LANES] = flag(
                iota((rcap[j], LANES), 0) + roff[j] == slots[me, k:k + 1, :]).astype(BF16)

        @pl.loop(0, width // 256)
        def _(n):
            cols = pl.ds(pl.multiple_of(n * 256, 256), 256)
            ret_out[roff[j]:roff[j + 1], cols] = jnp.dot(
                hot[0:rcap[j], 0:depth], contrib[0:depth, cols], preferred_element_type=F32).astype(BF16)

        back[j].start()

    def expert(e, carry):
        for i in range(GROUPS):
            pl.when(e == i * per_group)(functools.partial(arrive, i))
        rows = pl.ds(pl.multiple_of(e * cap, cap), cap)
        up_copy(e).wait()
        z = jnp.dot(picked[rows, :], up_buf[e % RING], preferred_element_type=F32)
        act = (0.5 * z * (1.0 + jnp.tanh(0.7978845608028654 * (z + 0.044715 * (z * z * z))))).astype(BF16)

        @pl.when(e + RING < experts)
        def _():
            up_copy(e + RING).start()

        down_copy(e).wait()
        for n in range(width // 512):
            cols = slice(n * 512, (n + 1) * 512)
            o = jnp.dot(act, down_buf[e % RING, :, cols], preferred_element_type=F32)
            contrib[rows, cols] = (o * gate_col[rows, :]).astype(BF16)

        @pl.when(e + RING < experts)
        def _():
            down_copy(e + RING).start()

        for j in range(GROUPS):
            pl.when(e == j * per_group + per_group - 1)(functools.partial(give, j))
        return carry

    lax.fori_loop(0, experts, expert, 0)

    def add_rows(d, source):
        for j in range(GROUPS):
            hot[:, j * LANES:(j + 1) * LANES] = flag(iota((tok, LANES), 0) + me * tok == sels[d, j:j + 1, :]).astype(BF16)

        @pl.loop(0, width // 256)
        def _(n):
            cols = pl.ds(pl.multiple_of(n * 256, 256), 256)
            acc[:, cols] += jnp.dot(hot[:, 0:GROUPS * LANES], source[:, cols], preferred_element_type=F32)

    def add_back(f, j):
        hot[:, 0:LANES] = flag(iota((tok, LANES), 0) + me * tok == toks[f, j]).astype(BF16)

        @pl.loop(0, width // 256)
        def _(n):
            cols = pl.ds(pl.multiple_of(n * 256, 256), 256)
            acc[:, cols] += jnp.dot(hot[:, 0:rcap[j]], ret_in[f, roff[j]:roff[j + 1], cols], preferred_element_type=F32)

    again = []
    for j in range(GROUPS):
        block = pl.ds(roff[j], rcap[j])
        again.append(remote(ret_in.at[0, block], ret_in.at[1, block], send_back.at[j], recv_back.at[j], near))

    add_rows(me, contrib)
    for j in range(GROUPS):
        pass_near[j].wait_recv()
    add_rows(near, contrib_near)
    for j in range(GROUPS):
        back[j].wait_recv()
        again[j].start()
        add_back(0, j)
        again[j].wait_recv()
        add_back(1, j)
    y_ref[...] = acc[...].astype(BF16)

    if checked:
        ok_send.wait()
        ok_ref[...] = ok_mine[...] * ok_other[...]
    else:
        ok_ref[...] = jnp.ones_like(ok_ref)
    to_near.wait_send()
    for copy in sel_send + link + forward + pass_near + back + again:
        copy.wait_send()


def solution(mesh):
    def layer(xcap, rcap, checked, collective_id, sel, gate, x_loc, up_loc, down_loc):
        tok, width = x_loc.shape
        experts, _, hidden = up_loc.shape
        vmem = pl.BlockSpec(memory_space=pltpu.VMEM)
        hbm = pl.BlockSpec(memory_space=pl.ANY)
        dma = pltpu.SemaphoreType.DMA
        entries = GROUPS * LANES
        four = dma((GROUPS,))
        return pl.pallas_call(
            functools.partial(moe_kernel, xcap, rcap, checked),
            out_shape=(jax.ShapeDtypeStruct((tok, width), BF16), jax.ShapeDtypeStruct((8, LANES), F32)),
            in_specs=[vmem, vmem, hbm, hbm, hbm],
            out_specs=(vmem, vmem),
            scratch_shapes=[
                pltpu.VMEM((2 * tok, width), BF16),
                pltpu.VMEM((sum(xcap) // 2, width), BF16),
                pltpu.VMEM((sum(xcap), width), BF16),
                pltpu.VMEM((entries, width), BF16),
                pltpu.VMEM((entries, width), BF16),
                pltpu.VMEM((entries, width), BF16),
                pltpu.VMEM((sum(rcap), width), BF16),
                pltpu.VMEM((2, sum(rcap), width), BF16),
                pltpu.VMEM((tok, width), F32),
                pltpu.VMEM((entries, 2 * tok), BF16),
                pltpu.VMEM((4, GROUPS, LANES), I32),
                pltpu.VMEM((4, GROUPS, LANES), I32),
                pltpu.VMEM((2, GROUPS, 1, LANES), I32),
                pltpu.VMEM((entries, 1), I32),
                pltpu.VMEM((entries, 1), F32),
                pltpu.VMEM((entries, 1), I32),
                pltpu.VMEM((8, LANES), I32),
                pltpu.VMEM((LANES, LANES), F32),
                pltpu.VMEM((8, LANES), F32),
                pltpu.VMEM((8, LANES), F32),
                pltpu.VMEM((RING, width, hidden), BF16),
                pltpu.VMEM((RING, hidden, width), BF16),
                dma, dma((RING,)), dma((RING,)), dma((3,)), dma((3,)), dma, dma,
                four, four, four, four, four, four, four, four, four, four, dma, dma,
            ],
            compiler_params=pltpu.CompilerParams(collective_id=collective_id, has_side_effects=True,
                                                 vmem_limit_bytes=64 * 1024 * 1024 - 65536),
        )(sel, gate, x_loc, up_loc, down_loc)

    def local_layer(x_loc, sel_loc, gate_loc, up_loc, down_loc):
        sel = sel_loc.reshape(GROUPS, LANES)
        gate = gate_loc.reshape(GROUPS, LANES)
        args = (sel, gate, x_loc, up_loc, down_loc)
        y, ok = layer((224, 128, 96, 96), (96, 96, 96, 128), True, 0, *args)
        return lax.cond(ok[0, 0] > 0.5, lambda: y, lambda: layer((256,) * 4, (128,) * 4, False, 1, *args)[0])

    row_spec = P(("dp", "ep"), None)
    weight_spec = P("ep", None, None)
    return jax.shard_map(local_layer, mesh=mesh, in_specs=(row_spec, row_spec, row_spec, weight_spec, weight_spec), out_specs=row_spec, check_vma=False)
```

time: 233 us -> 95.9 us (0.41)
  waiting for transfers between devices: 93 us -> 0 us
  Pallas kernels: 0 us -> 87.7 us
  matrix products: 47.7 us -> 0 us
  other arithmetic: 44 us -> 0 us
  local copies, waits for them, and re-layouts: 29 us -> 7.04 us
  starting transfers between devices: 10 us -> 0 us
  blocking collectives: 8.21 us -> 0 us
    all_to_all x2 -> x0, waiting for transfers between devices: 93 us -> none  [the longest x1 47.6 us: local_layer(): lax.all_to_all(send_rows, 'ep', 0, 0, tiled=True)]
    pallas_call x0 -> x1, Pallas kernels: none -> 87.7 us  [layer(): pl.pallas_call(functools.partial(moe_kernel, xcap, rcap, checked), out_sh...]
    dot_general x2 -> x0, matrix products: 47.7 us -> none  [the longest x1 24.1 us: local_layer(): jnp.einsum('ecd,edf->ecf', picked, up_loc, preferred_element_type=jnp.flo...]
    scatter-add x2 -> x0, other arithmetic: 22.8 us -> none  [the longest x1 18.7 us: local_layer(): jax.ops.segment_sum(returned.astype(jnp.float32), wanted, num_segments=to...]
    gather x3 -> x0, local copies, waits for them, and re-layouts: 18.5 us -> none  [the longest x1 10.7 us: local_layer(): jnp.take(x_loc, wanted, axis=0).reshape(group_size, pair_cap, model_width)]
    all_to_all x2 -> x0, starting transfers between devices: 10 us -> none  [the longest x1 5.02 us: local_layer(): lax.all_to_all(send_rows, 'ep', 0, 0, tiled=True)]
    scatter x2 -> x0, local copies, waits for them, and re-layouts: 8.89 us -> none  [the longest x1 6.45 us: local_layer(): jnp.zeros((group_size * pair_cap, model_width), jnp.bfloat16).at[slot_idx]]
    all_to_all x1 -> x0, blocking collectives: 8.21 us -> none  [local_layer(): lax.all_to_all(request.reshape(group_size, pair_cap), 'ep', 0, 0, tiled=T...]
  transfers between devices with their start and end apart: 2 -> 0, of which waited for: 2 -> 0; matrix products, arithmetic and copies ran while one was open for 1% -> 0% of each run, Pallas kernels for 0% -> 0%
where the time goes in v2:
time: 95.9 us; the launch traced here: 95.6 us
  Pallas kernels  87.7 us (91%)
  local copies, waits for them, and re-layouts  7.04 us (7%)
    pallas_call x1, Pallas kernels, layer(): pl.pallas_call(functools.partial(moe_kernel, xcap, rcap, checked), out_sh...  87.7 us
    unnamed x1, local copies, waits for them, and re-layouts  3.16 us

profile of v2, /device:TPU:0, one launch (start us, length us, event | category | flops | bytes accessed | tf_op | source)
XLA Modules:
  0.0 95.6 jit_solution(12315062601580346731)
XLA Ops:
  0.0 1.4 %reshape.10.sel_in = s32[4,128]{1,0:T(4,128)} reshape(s32[16,32]{1,0:T(8,128)} %param.8) | data formatting | bytes 4096 | tf_op jit(solution)/shard_map/reshape | solution.py:351
  1.4 1.3 %reshape.11.gate_in = f32[4,128]{1,0:T(4,128)} reshape(f32[16,32]{1,0:T(8,128)} %param.9) | data formatting | bytes 4096 | tf_op jit(solution)/shard_map/reshape | solution.py:352
  2.7 87.7 %shard_map.57 = (bf16[512,2048]{1,0:T(8,128)(2,1)}, f32[8,128]{1,0:T(8,128)}) custom-call(s32[4,128]{1,0:T(4,128)} %reshape.10.sel_in, f32[4,128]{1,0:T(4,128)} %reshape.11.gate_in, bf16[512,2048]{1,0:T(8,128)(2,1)} %x_hbm.1, bf16[16,2048,1024]{2,1,0:T(8,128)(2,1)} %up_hbm.1, bf16[16,1024,2048]{2,1,0:T(8,128)(2,1)} %down_hbm.1), custom_call_target="tpu_custom_call" | custom-call | tf_op jit(solution)/shard_map/pallas_call | solution.py:315
  90.4 1.2 %slice.3 = f32[1,1]{1,0:T(1,128)} slice(f32[8,128]{1,0:T(8,128)} %get-tuple-element.27), slice={[0:1], [0:1]} | slice | bytes 8 | tf_op jit(solution)/shard_map/slice | solution.py:355
  92.2 0.2 conditional.1
  92.4 3.2 %copy.11 = bf16[512,2048]{1,0:T(8,128)(2,1)} copy(bf16[512,2048]{1,0:T(8,128)(2,1)} %get-tuple-element.29) | data formatting | bytes 4194304

commit v3 on v2

--- a/solution.py
+++ b/solution.py
@@ -143,10 +143,7 @@
             hot[0:part, b * LANES:(b + 1) * LANES] = flag(iota((part, LANES), 0) + start == pos_out[b:b + 1, :]).astype(BF16)
         at = pl.ds(xoff[i] // 2, part)
 
-        @pl.loop(0, width // 256)
-        def _(n):
-            cols = pl.ds(pl.multiple_of(n * 256, 256), 256)
-            x_out[at, cols] = jnp.dot(hot[0:part, 0:2 * tok], x_chip[:, cols], preferred_element_type=F32).astype(BF16)
+        x_out[at, :] = jnp.dot(hot[0:part, 0:2 * tok], x_chip[:, :], preferred_element_type=F32).astype(BF16)
 
         link.append(remote(x_out.at[at], x_in.at[pl.ds(pl.multiple_of(start, 16), part)], send_link.at[i], recv_link.at[i], far))
         link[i].start()
@@ -166,10 +163,7 @@
         base = chip * (2 * tok) + b * LANES
         hot[:, b * LANES:(b + 1) * LANES] = flag(sel_col[...] == iota((GROUPS * LANES, LANES), 1) + base).astype(BF16)
 
-    @pl.loop(0, width // 256)
-    def _(n):
-        cols = pl.ds(pl.multiple_of(n * 256, 256), 256)
-        picked[:, cols] = jnp.dot(hot[:, 0:2 * tok], x_chip[:, cols], preferred_element_type=F32).astype(BF16)
+    picked[:, :] = jnp.dot(hot[:, 0:2 * tok], x_chip[:, :], preferred_element_type=F32).astype(BF16)
 
     for f, d in enumerate((far, diag)):
         row = sels[d]
@@ -203,11 +197,8 @@
         hot[r0:, 0:size] = flag(need_col[r0:, :] == iota((GROUPS * LANES - r0, size), 1) + xoff[i]).astype(BF16)
         forward[i].wait_recv()
 
-        @pl.loop(0, width // 256)
-        def _(n):
-            cols = pl.ds(pl.multiple_of(n * 256, 256), 256)
-            picked[r0:, cols] = picked[r0:, cols] + jnp.dot(
-                hot[r0:, 0:size], x_in[xoff[i]:xoff[i + 1], cols], preferred_element_type=F32).astype(BF16)
+        picked[r0:, :] = picked[r0:, :] + jnp.dot(
+            hot[r0:, 0:size], x_in[xoff[i]:xoff[i + 1], :], preferred_element_type=F32).astype(BF16)
 
     pass_near, back = [], []
     for j in range(GROUPS):
@@ -223,11 +214,8 @@
             hot[0:rcap[j], k * LANES:(k + 1) * LANES] = flag(
                 iota((rcap[j], LANES), 0) + roff[j] == slots[me, k:k + 1, :]).astype(BF16)
 
-        @pl.loop(0, width // 256)
-        def _(n):
-            cols = pl.ds(pl.multiple_of(n * 256, 256), 256)
-            ret_out[roff[j]:roff[j + 1], cols] = jnp.dot(
-                hot[0:rcap[j], 0:depth], contrib[0:depth, cols], preferred_element_type=F32).astype(BF16)
+        ret_out[roff[j]:roff[j + 1], :] = jnp.dot(
+            hot[0:rcap[j], 0:depth], contrib[0:depth, :], preferred_element_type=F32).astype(BF16)
 
         back[j].start()
 
@@ -263,18 +251,12 @@
         for j in range(GROUPS):
             hot[:, j * LANES:(j + 1) * LANES] = flag(iota((tok, LANES), 0) + me * tok == sels[d, j:j + 1, :]).astype(BF16)
 
-        @pl.loop(0, width // 256)
-        def _(n):
-            cols = pl.ds(pl.multiple_of(n * 256, 256), 256)
-            acc[:, cols] += jnp.dot(hot[:, 0:GROUPS * LANES], source[:, cols], preferred_element_type=F32)
+        acc[:, :] += jnp.dot(hot[:, 0:GROUPS * LANES], source[:, :], preferred_element_type=F32)
 
     def add_back(f, j):
         hot[:, 0:LANES] = flag(iota((tok, LANES), 0) + me * tok == toks[f, j]).astype(BF16)
 
-        @pl.loop(0, width // 256)
-        def _(n):
-            cols = pl.ds(pl.multiple_of(n * 256, 256), 256)
-            acc[:, cols] += jnp.dot(hot[:, 0:rcap[j]], ret_in[f, roff[j]:roff[j + 1], cols], preferred_element_type=F32)
+        acc[:, :] += jnp.dot(hot[:, 0:rcap[j]], ret_in[f, roff[j]:roff[j + 1], :], preferred_element_type=F32)
 
     again = []
     for j in range(GROUPS):

time: 95.9 us -> 83.8 us (0.87)
  Pallas kernels: 87.7 us -> 75.8 us
    pallas_call x1, Pallas kernels: 87.7 us -> 75.8 us  [layer(): pl.pallas_call(functools.partial(moe_kernel, xcap, rcap, checked), out_sh...]
where the time goes in v3:
time: 83.8 us; the launch traced here: 83.5 us
  Pallas kernels  75.8 us (90%)
  local copies, waits for them, and re-layouts  7.04 us (8%)
    pallas_call x1, Pallas kernels, layer(): pl.pallas_call(functools.partial(moe_kernel, xcap, rcap, checked), out_sh...  75.8 us
    unnamed x1, local copies, waits for them, and re-layouts  3.16 us

profile of v3, /device:TPU:0, one launch (start us, length us, event | category | flops | bytes accessed | tf_op | source)
XLA Modules:
  0.0 83.5 jit_solution(6381402422552477027)
XLA Ops:
  0.0 1.4 %reshape.10.sel_in = s32[4,128]{1,0:T(4,128)} reshape(s32[16,32]{1,0:T(8,128)} %param.8) | data formatting | bytes 4096 | tf_op jit(solution)/shard_map/reshape | solution.py:333
  1.4 1.3 %reshape.11.gate_in = f32[4,128]{1,0:T(4,128)} reshape(f32[16,32]{1,0:T(8,128)} %param.9) | data formatting | bytes 4096 | tf_op jit(solution)/shard_map/reshape | solution.py:334
  2.7 75.8 %shard_map.57 = (bf16[512,2048]{1,0:T(8,128)(2,1)}, f32[8,128]{1,0:T(8,128)}) custom-call(s32[4,128]{1,0:T(4,128)} %reshape.10.sel_in, f32[4,128]{1,0:T(4,128)} %reshape.11.gate_in, bf16[512,2048]{1,0:T(8,128)(2,1)} %x_hbm.1, bf16[16,2048,1024]{2,1,0:T(8,128)(2,1)} %up_hbm.1, bf16[16,1024,2048]{2,1,0:T(8,128)(2,1)} %down_hbm.1), custom_call_target="tpu_custom_call" | custom-call | tf_op jit(solution)/shard_map/pallas_call | solution.py:297
  78.6 1.2 %slice.3 = f32[1,1]{1,0:T(1,128)} slice(f32[8,128]{1,0:T(8,128)} %get-tuple-element.27), slice={[0:1], [0:1]} | slice | bytes 8 | tf_op jit(solution)/shard_map/slice | solution.py:337
  80.3 3.2 %copy.11 = bf16[512,2048]{1,0:T(8,128)(2,1)} copy(bf16[512,2048]{1,0:T(8,128)(2,1)} %get-tuple-element.29) | data formatting | bytes 4194304
  (1 shorter events, 0.0 us)

commit v4 on v0

v4 whole, which is shorter than its diff:
```python
import functools

import jax
import jax.numpy as jnp
from jax import lax
from jax.experimental import pallas as pl
from jax.experimental.pallas import tpu as pltpu
from jax.sharding import PartitionSpec as P

MESH = pl.DeviceIdType.MESH
GROUPS = 4
LANES = 128
ENTRIES = GROUPS * LANES
BF16 = jnp.bfloat16
F32 = jnp.float32
I32 = jnp.int32
SENT_AFTER = (None, None, 3, 7, 11, 13, 15)
CHUNKS = len(SENT_AFTER)
FIT = dict(sizes=(112, 64, 80, 96, 96, 48, 80), ring=3, step=2048, checked=True)
FULL = dict(sizes=(128, 128, 256, 256, 128, 64, 64), ring=2, step=512, checked=False)


def iota(shape, dim):
    return lax.broadcasted_iota(I32, shape, dim)


def mm(a, b):
    return jnp.dot(a.astype(BF16), b.astype(BF16), preferred_element_type=F32)


def mm_t(a, b):
    return lax.dot_general(a.astype(BF16), b.astype(BF16), (((1,), (1,)), ((), ())), preferred_element_type=F32)


def flag(cond):
    return jnp.where(cond, 1.0, 0.0)


def total(a):
    return jnp.sum(jnp.sum(a, axis=1, keepdims=True), axis=0, keepdims=True)


def plan(sizes):
    off = [sum(sizes[:c]) for c in range(CHUNKS + 1)]
    base = [2 * off[c] + (2 * ENTRIES if c >= 2 else 0) for c in range(CHUNKS + 1)]
    return off, base, 2 * off[2], 2 * off[2] + ENTRIES


def moe_kernel(sizes, ring, step, checked, sel_in, gate_in, x_hbm, up_hbm, down_hbm, y_ref, ok_ref,
               x_chip, out, rows_in, picked, acc, hot,
               sel_row, sels, slots, toks_a, toks_b, sel_col, gate_col, need_col, pos_out, square, ok_mine, ok_other,
               up_buf, down_buf,
               x_sem, up_sem, down_sem, send_sel, recv_sel, send_x, recv_x, send_link, recv_link, send_fwd, recv_fwd,
               send_near, recv_near, send_ok, recv_ok):
    tok, width = y_ref.shape
    experts, cap = sel_in.shape
    per_group = experts // GROUPS
    off, base, own_at, near_at = plan(sizes)
    me = lax.axis_index("ep")
    core = me % 2
    chip = me // 2
    near = me + 1 - 2 * core
    far = (me + 2) % 4
    diag = 3 - me
    peers = (near, far, diag)
    other_group = 1 - lax.axis_index("dp")

    def up_copy(e):
        return pltpu.make_async_copy(up_hbm.at[e], up_buf.at[e % ring], up_sem.at[e % ring])

    def down_copy(e):
        return pltpu.make_async_copy(down_hbm.at[e], down_buf.at[e % ring], down_sem.at[e % ring])

    def remote(src, dst, send, recv, peer, axis="ep"):
        return pltpu.make_async_remote_copy(src_ref=src, dst_ref=dst, send_sem=send, recv_sem=recv,
                                            device_id={axis: peer}, device_id_type=MESH)

    def by_columns(write):
        if step == width:
            write(slice(None))
        else:
            @pl.loop(0, width // step)
            def _(n):
                write(pl.ds(pl.multiple_of(n * step, step), step))

    own_rows = pl.ds(pl.multiple_of(core * tok, tok), tok)
    load_x = pltpu.make_async_copy(x_hbm, x_chip.at[own_rows], x_sem)
    load_x.start()

    barrier = pltpu.get_barrier_semaphore()
    for peer in peers:
        pl.semaphore_signal(barrier, inc=1, device_id={"ep": peer}, device_id_type=MESH)
    if checked:
        pl.semaphore_signal(barrier, inc=1, device_id={"dp": other_group}, device_id_type=MESH)
    for e in range(ring):
        up_copy(e).start()
        down_copy(e).start()

    spread = flag(iota((cap, LANES), 0) == iota((cap, LANES), 1) % cap)
    inside = flag(iota((experts, LANES), 0) % per_group == iota((experts, LANES), 1) // cap)
    gather = flag(iota((GROUPS, experts), 1) // per_group == iota((GROUPS, experts), 0))
    high = mm(gather, mm((sel_in[...] >> 5).astype(F32), spread) * inside)
    low = mm(gather, mm((sel_in[...] & 31).astype(F32), spread) * inside)
    sel_row[...] = (high * 32.0 + low).astype(I32)
    square[...] = jnp.zeros_like(square)
    square[0:experts, 0:cap] = sel_in[...].astype(F32)
    square[experts:2 * experts, 0:cap] = gate_in[...]
    turned = square[...].T
    for e in range(experts):
        sel_col[e * cap:(e + 1) * cap, :] = turned[0:cap, e:e + 1].astype(I32)
        gate_col[e * cap:(e + 1) * cap, :] = turned[0:cap, experts + e:experts + e + 1]

    pl.semaphore_wait(barrier, 4 if checked else 3)
    sel_send = [remote(sel_row, sels.at[me], send_sel.at[i], recv_sel.at[i], peer) for i, peer in enumerate(peers)]
    for copy in sel_send:
        copy.start()
    load_x.wait()
    to_near = remote(x_chip.at[own_rows], x_chip.at[own_rows], send_x, recv_x, near)
    to_near.start()
    sels[me] = sel_row[...]

    before = flag(iota((LANES, LANES), 0) < iota((LANES, LANES), 1))
    ones = jnp.ones((LANES, LANES), F32)
    rows_before = flag(iota((GROUPS * 8, GROUPS * 8), 1) < iota((GROUPS * 8, GROUPS * 8), 0))
    for copy in sel_send:
        copy.wait_recv()

    def row_order(c):
        start = (1 - c) * (2 * tok)
        seen = jnp.zeros((8, LANES), F32)
        firsts, fit = [], jnp.ones((1, 1), F32)
        for j in range(GROUPS):
            row = jnp.concatenate([sels[2 * c, j:j + 1, :], sels[2 * c + 1, j:j + 1, :]], axis=1) - start
            row_high = flag(iota((8, 2 * LANES), 0) == (row >> 7))
            row_low = flag(iota((LANES, 2 * LANES), 0) == (row & 127))
            need = flag(mm_t(row_high, row_low) > 0.5)
            firsts.append(need * (1.0 - seen))
            seen = jnp.maximum(seen, need)
            fit = fit * flag(total(seen) < 2.0 * off[j + 1] + 0.5)
        first = jnp.concatenate(firsts, axis=0)
        place = mm(first, before) + mm(rows_before, mm(first, ones))
        pos = sum(firsts[j] * (place[8 * j:8 * j + 8] + 1.0) for j in range(GROUPS)) - 1.0
        return pos.astype(I32), total(seen), fit

    def entry_order(d, sent_rows):
        away = flag((sels[d] >> 10) != d // 2)
        rank = mm(away, before)
        lane = iota((GROUPS, LANES), 1)
        early = flag(lane < LANES // 2)
        count = jnp.sum(away, axis=1, keepdims=True)
        count_early = jnp.sum(away * early, axis=1, keepdims=True)
        end = jnp.floor((sent_rows + 1.0) * 0.5)
        for j in range(GROUPS):
            row = slice(j, j + 1)
            begin = jnp.maximum(end, float(off[j + 2]))
            place = rank[row] + begin
            end = begin + count[row]
            if j == GROUPS - 1:
                later = jnp.maximum(begin + count_early[row], float(off[CHUNKS - 1]))
                place = jnp.where(lane[row] < LANES // 2, place, rank[row] - count_early[row] + later)
                end = later + count[row] - count_early[row]
            slots[d, row, :] = (away[row] * (place + 1.0) - 1.0).astype(I32)
        return flag(end < off[CHUNKS] + 0.5)

    pos, rows_sent, fit = row_order(1 - chip)
    pos_out[...] = jnp.where((pos & 1) == core, pos >> 1, -1)
    to_near.wait_recv()

    def pack(lo, hi):
        size = off[hi] - off[lo]
        for b in range(8):
            hot[0:size, b * LANES:(b + 1) * LANES] = flag(iota((size, LANES), 0) + off[lo] == pos_out[b:b + 1, :]).astype(BF16)

        def write(cols):
            out[off[lo]:off[hi], cols] = jnp.dot(hot[0:size, 0:2 * tok], x_chip[:, cols],
                                                 preferred_element_type=F32).astype(BF16)
        by_columns(write)

    link, forward = [], []
    for c in range(CHUNKS):
        mine = rows_in.at[pl.ds(base[c], sizes[c])]
        theirs = rows_in.at[pl.ds(base[c] + sizes[c], sizes[c])]
        link.append(remote(out.at[pl.ds(off[c], sizes[c])], mine, send_link.at[c], recv_link.at[c], far))
        forward.append(remote(mine, theirs, send_fwd.at[c], recv_fwd.at[c], near))
    pass_near = []
    for j in range(GROUPS):
        pass_near.append(remote(rows_in.at[pl.ds(own_at + j * LANES, LANES)], rows_in.at[pl.ds(near_at + j * LANES, LANES)],
                                send_near.at[j], recv_near.at[j], near))

    pack(0, 2)
    link[0].start()
    link[1].start()
    pack(2, 4)

    wanted, rows_got, fit_in = row_order(chip)
    fit = fit * fit_in
    for d in range(4):
        same_chip = flag(jnp.full((1, 1), d // 2, I32) == chip)
        fit = fit * entry_order(d, same_chip * rows_sent + (1.0 - same_chip) * rows_got)

    slot = wanted >> 1
    side = jnp.where((wanted & 1) == core, 0, 1)
    where_in = jnp.full((8, LANES), -1, I32)
    for c in range(GROUPS):
        here = (slot >= off[c]) & (slot < off[c + 1]) & (wanted >= 0)
        where_in = jnp.where(here, base[c] - off[c] + slot + side * sizes[c], where_in)
    where_in = where_in.astype(F32)
    found = jnp.zeros((ENTRIES, LANES), F32)
    for b in range(8):
        start = (1 - chip) * (2 * tok) + b * LANES
        found = found + jnp.where(sel_col[...] == iota((ENTRIES, LANES), 1) + start, where_in[b:b + 1, :] + 1.0, 0.0)
    need_col[...] = (jnp.sum(found, axis=1, keepdims=True) - 1.0).astype(I32)

    for b in range(8):
        start = chip * (2 * tok) + b * LANES
        hot[0:ENTRIES, b * LANES:(b + 1) * LANES] = flag(sel_col[...] == iota((ENTRIES, LANES), 1) + start).astype(BF16)

    def pick_local(cols):
        picked[:, cols] = jnp.dot(hot[0:ENTRIES, 0:2 * tok], x_chip[:, cols], preferred_element_type=F32).astype(BF16)
    by_columns(pick_local)

    values = []
    for d in (far, diag):
        for k in range(GROUPS):
            at = iota((8, LANES), 0)
            row = sels[d, k:k + 1, :]
            values.append(jnp.where(at == 0, row >> 5, jnp.where(at == 1, row & 31, 1)).astype(F32))
    values = jnp.concatenate(values, axis=1)
    for c in range(2, CHUNKS):
        size = sizes[c]
        at = iota((2 * size, LANES), 0)
        for f, d in enumerate((far, diag)):
            key = jnp.where((at >= f * size) & (at < (f + 1) * size), at - f * size + off[c], -2)
            for k in range(GROUPS):
                block = (f * GROUPS + k) * LANES
                hot[0:2 * size, block:block + LANES] = flag(key == slots[d, k:k + 1, :]).astype(BF16)
        sums = mm_t(values, hot[0:2 * size, 0:2 * ENTRIES])
        token = jnp.where(sums[2:3] > 0.5, sums[0:1] * 32.0 + sums[1:2], -1.0).astype(I32)
        if c < 5:
            toks_a[:, base[c] - base[2]:base[c + 1] - base[2]] = token
        else:
            toks_b[:, base[c] - base[5]:base[c + 1] - base[5]] = token

    if checked:
        ok_mine[...] = jnp.broadcast_to(fit, ok_mine.shape)
        ok_send = remote(ok_mine, ok_other, send_ok, recv_ok, other_group, "dp")
        ok_send.start()

    def arrive(c):
        link[c].wait_recv()
        forward[c].start()
        r0, size = c * LANES, 2 * sizes[c]
        hot[r0:ENTRIES, 0:size] = flag(need_col[r0:, :] == iota((ENTRIES - r0, size), 1) + base[c]).astype(BF16)
        forward[c].wait_recv()

        def write(cols):
            picked[r0:, cols] = picked[r0:, cols] + jnp.dot(
                hot[r0:ENTRIES, 0:size], rows_in[base[c]:base[c] + size, cols], preferred_element_type=F32).astype(BF16)
        by_columns(write)

    def give(c):
        size = sizes[c]
        depth = (SENT_AFTER[c] + 1) * cap
        for k in range(0, depth, LANES):
            part = min(LANES, depth - k)
            row = slots[me, k // LANES:k // LANES + 1, 0:part]
            hot[0:size, k:k + part] = flag(iota((size, part), 0) + off[c] == row).astype(BF16)

        def write(cols):
            packed = jnp.dot(hot[0:size, 0:depth], rows_in[own_at:own_at + depth, cols],
                             preferred_element_type=F32).astype(BF16)
            if c < GROUPS:
                packed = packed + out[off[c]:off[c + 1], cols]
            out[off[c]:off[c + 1], cols] = packed
        by_columns(write)
        link[c].start()

    def expert(e, carry):
        for c in range(GROUPS):
            pl.when(e == c * per_group)(functools.partial(arrive, c))
        rows = pl.ds(pl.multiple_of(e * cap, cap), cap)
        own = pl.ds(pl.multiple_of(own_at + e * cap, 32), cap)
        up_copy(e).wait()
        z = jnp.dot(picked[rows, :], up_buf[e % ring], preferred_element_type=F32)
        act = (0.5 * z * (1.0 + jnp.tanh(0.7978845608028654 * (z + 0.044715 * (z * z * z))))).astype(BF16)

        @pl.when(e + ring < experts)
        def _():
            up_copy(e + ring).start()

        down_copy(e).wait()
        for n in range(width // 512):
            cols = slice(n * 512, (n + 1) * 512)
            o = jnp.dot(act, down_buf[e % ring, :, cols], preferred_element_type=F32)
            rows_in[own, cols] = (o * gate_col[rows, :]).astype(BF16)

        @pl.when(e + ring < experts)
        def _():
            down_copy(e + ring).start()

        for c in range(2, CHUNKS):
            pl.when(e == SENT_AFTER[c])(functools.partial(give, c))
        for j in range(GROUPS):
            pl.when(e == j * per_group + per_group - 1)(pass_near[j].start)
        return carry

    lax.fori_loop(0, experts, expert, 0)

    link[4].wait_recv()
    forward[4].start()
    early = base[5] - own_at
    for at, d in ((0, me), (ENTRIES, near)):
        for k in range(GROUPS):
            hot[0:tok, at + k * LANES:at + (k + 1) * LANES] = flag(
                iota((tok, LANES), 0) + me * tok == sels[d, k:k + 1, :]).astype(BF16)
    hot[0:tok, 2 * ENTRIES:early] = flag(iota((tok, early - 2 * ENTRIES), 0) + me * tok == toks_a[...]).astype(BF16)
    for copy in pass_near:
        copy.wait_recv()
    forward[4].wait_recv()

    def add_early(cols):
        acc[:, cols] = x_chip[own_rows, cols].astype(F32) + jnp.dot(
            hot[0:tok, 0:early], rows_in[own_at:base[5], cols], preferred_element_type=F32)
    by_columns(add_early)

    late = base[CHUNKS] - base[5]
    for c in (5, 6):
        link[c].wait_recv()
        forward[c].start()
    hot[0:tok, 0:late] = flag(iota((tok, late), 0) + me * tok == toks_b[...]).astype(BF16)
    for c in (5, 6):
        forward[c].wait_recv()

    def add_late(cols):
        y_ref[:, cols] = (acc[:, cols] + jnp.dot(hot[0:tok, 0:late], rows_in[base[5]:base[CHUNKS], cols],
                                                 preferred_element_type=F32)).astype(BF16)
    by_columns(add_late)

    if checked:
        ok_send.wait()
        ok_ref[0, 0] = jnp.min(ok_mine[...] * ok_other[...])
    else:
        ok_ref[0, 0] = 1.0
    to_near.wait_send()
    for copy in sel_send + link + forward + pass_near:
        copy.wait_send()


def solution(mesh):
    def layer(sizes, ring, step, checked, collective_id, sel, gate, x_loc, up_loc, down_loc):
        tok, width = x_loc.shape
        experts, _, hidden = up_loc.shape
        off, base, own_at, _ = plan(sizes)
        vmem = pl.BlockSpec(memory_space=pltpu.VMEM)
        hbm = pl.BlockSpec(memory_space=pl.ANY)
        dma = pltpu.SemaphoreType.DMA
        each = dma((CHUNKS,))
        return pl.pallas_call(
            functools.partial(moe_kernel, sizes, ring, step, checked),
            out_shape=(jax.ShapeDtypeStruct((tok, width), BF16), jax.ShapeDtypeStruct((1, 1), F32)),
            in_specs=[vmem, vmem, hbm, hbm, hbm],
            out_specs=(vmem, pl.BlockSpec(memory_space=pltpu.SMEM)),
            scratch_shapes=[
                pltpu.VMEM((2 * tok, width), BF16),
                pltpu.VMEM((off[CHUNKS], width), BF16),
                pltpu.VMEM((base[CHUNKS], width), BF16),
                pltpu.VMEM((ENTRIES, width), BF16),
                pltpu.VMEM((tok, width), F32),
                pltpu.VMEM((tok, max(2 * tok, base[5] - own_at)), BF16),
                pltpu.VMEM((GROUPS, LANES), I32),
                pltpu.VMEM((4, GROUPS, LANES), I32),
                pltpu.VMEM((4, GROUPS, LANES), I32),
                pltpu.VMEM((1, base[5] - base[2]), I32),
                pltpu.VMEM((1, base[CHUNKS] - base[5]), I32),
                pltpu.VMEM((ENTRIES, 1), I32),
                pltpu.VMEM((ENTRIES, 1), F32),
                pltpu.VMEM((ENTRIES, 1), I32),
                pltpu.VMEM((8, LANES), I32),
                pltpu.VMEM((LANES, LANES), F32),
                pltpu.VMEM((8, LANES), F32),
                pltpu.VMEM((8, LANES), F32),
                pltpu.VMEM((ring, width, hidden), BF16),
                pltpu.VMEM((ring, hidden, width), BF16),
                dma, dma((ring,)), dma((ring,)), dma((3,)), dma((3,)), dma, dma,
                each, each, each, each, dma((GROUPS,)), dma((GROUPS,)), dma, dma,
            ],
            compiler_params=pltpu.CompilerParams(collective_id=collective_id, has_side_effects=True,
                                                 vmem_limit_bytes=64 * 1024 * 1024 - 65536),
        )(sel, gate, x_loc, up_loc, down_loc)

    def local_layer(x_loc, sel_loc, gate_loc, up_loc, down_loc):
        args = (sel_loc, gate_loc, x_loc, up_loc, down_loc)
        y, ok = layer(*FIT.values(), 0, *args)
        return lax.cond(ok[0, 0] > 0.5, lambda: y, lambda: layer(*FULL.values(), 1, *args)[0])

    row_spec = P(("dp", "ep"), None)
    weight_spec = P("ep", None, None)
    return jax.shard_map(local_layer, mesh=mesh, in_specs=(row_spec, row_spec, row_spec, weight_spec, weight_spec), out_specs=row_spec, check_vma=False)
```

time: 233 us -> 79.1 us (0.34)
  waiting for transfers between devices: 93 us -> 0 us
  Pallas kernels: 0 us -> 75.1 us
  matrix products: 47.7 us -> 0 us
  other arithmetic: 44 us -> 0 us
  local copies, waits for them, and re-layouts: 29 us -> 3.16 us
  starting transfers between devices: 10 us -> 0 us
  blocking collectives: 8.21 us -> 0 us
    all_to_all x2 -> x0, waiting for transfers between devices: 93 us -> none  [the longest x1 47.6 us: local_layer(): lax.all_to_all(send_rows, 'ep', 0, 0, tiled=True)]
    pallas_call x0 -> x1, Pallas kernels: none -> 75.1 us  [layer(): pl.pallas_call(functools.partial(moe_kernel, sizes, ring, step, checked),...]
    dot_general x2 -> x0, matrix products: 47.7 us -> none  [the longest x1 24.1 us: local_layer(): jnp.einsum('ecd,edf->ecf', picked, up_loc, preferred_element_type=jnp.flo...]
    scatter-add x2 -> x0, other arithmetic: 22.8 us -> none  [the longest x1 18.7 us: local_layer(): jax.ops.segment_sum(returned.astype(jnp.float32), wanted, num_segments=to...]
    gather x3 -> x0, local copies, waits for them, and re-layouts: 18.5 us -> none  [the longest x1 10.7 us: local_layer(): jnp.take(x_loc, wanted, axis=0).reshape(group_size, pair_cap, model_width)]
    all_to_all x2 -> x0, starting transfers between devices: 10 us -> none  [the longest x1 5.02 us: local_layer(): lax.all_to_all(send_rows, 'ep', 0, 0, tiled=True)]
    scatter x2 -> x0, local copies, waits for them, and re-layouts: 8.89 us -> none  [the longest x1 6.45 us: local_layer(): jnp.zeros((group_size * pair_cap, model_width), jnp.bfloat16).at[slot_idx]]
    all_to_all x1 -> x0, blocking collectives: 8.21 us -> none  [local_layer(): lax.all_to_all(request.reshape(group_size, pair_cap), 'ep', 0, 0, tiled=T...]
  transfers between devices with their start and end apart: 2 -> 0, of which waited for: 2 -> 0; matrix products, arithmetic and copies ran while one was open for 1% -> 0% of each run, Pallas kernels for 0% -> 0%
where the time goes in v4:
time: 79.1 us; the launch traced here: 78.9 us
  Pallas kernels  75.1 us (95%)
  local copies, waits for them, and re-layouts  3.16 us (4%)
    pallas_call x1, Pallas kernels, layer(): pl.pallas_call(functools.partial(moe_kernel, sizes, ring, step, checked),...  75.1 us
    unnamed x1, local copies, waits for them, and re-layouts  3.16 us

profile of v4, /device:TPU:0, one launch (start us, length us, event | category | flops | bytes accessed | tf_op | source)
XLA Modules:
  0.0 78.9 jit_solution(15537983448879207996)
XLA Ops:
  0.0 75.1 %shard_map.57 = (bf16[512,2048]{1,0:T(8,128)(2,1)}, f32[1,1]{1,0:T(1,128)}) custom-call(s32[16,32]{1,0:T(8,128)} %sel_in.1, f32[16,32]{1,0:T(8,128)} %gate_in.1, bf16[512,2048]{1,0:T(8,128)(2,1)} %x_hbm.1, bf16[16,2048,1024]{2,1,0:T(8,128)(2,1)} %up_hbm.1, bf16[16,1024,2048]{2,1,0:T(8,128)(2,1)} %down_hbm.1), custom_call_target="tpu_custom_call" | custom-call | tf_op jit(solution)/shard_map/pallas_call | solution.py:358
  75.7 3.2 %copy.11 = bf16[512,2048]{1,0:T(8,128)(2,1)} copy(bf16[512,2048]{1,0:T(8,128)(2,1)} %get-tuple-element.29) | data formatting | bytes 4194304
  (1 shorter events, 0.0 us)

commit v5 on v4

--- a/solution.py
+++ b/solution.py
@@ -14,10 +14,16 @@
 BF16 = jnp.bfloat16
 F32 = jnp.float32
 I32 = jnp.int32
-SENT_AFTER = (None, None, 3, 7, 11, 13, 15)
+SENT_AFTER = (None, None, None, None, 1, 3, 5, 7, 9, 11, 13, 15)
 CHUNKS = len(SENT_AFTER)
-FIT = dict(sizes=(112, 64, 80, 96, 96, 48, 80), ring=3, step=2048, checked=True)
-FULL = dict(sizes=(128, 128, 256, 256, 128, 64, 64), ring=2, step=512, checked=False)
+FIRST = 4
+X_FROM = (0, 2, 4, 6, 8, 12, 16)
+X_LAST = (0, 1, 2, 3, 4, 6)
+XGROUPS = len(X_LAST)
+XCHUNKS = X_LAST[-1] + 1
+LATE = CHUNKS - 2
+FIT = dict(sizes=(64, 48, 32, 32, 48, 32, 48, 48, 48, 48, 64, 64), ring=3, step=2048, checked=True)
+FULL = dict(sizes=(64, 64, 64, 64, 128, 64, 64, 192, 128, 64, 64, 64), ring=2, step=512, checked=False)
 
 
 def iota(shape, dim):
@@ -42,13 +48,21 @@
 
 def plan(sizes):
     off = [sum(sizes[:c]) for c in range(CHUNKS + 1)]
-    base = [2 * off[c] + (2 * ENTRIES if c >= 2 else 0) for c in range(CHUNKS + 1)]
-    return off, base, 2 * off[2], 2 * off[2] + ENTRIES
+    near_at = [2 * off[FIRST] + j * LANES for j in range(GROUPS - 1)]
+    shift = (GROUPS - 1) * LANES
+    own_at = 2 * off[XCHUNKS] + shift
+    near_at.append(own_at + ENTRIES)
+    base = [2 * off[c] + (0 if c < FIRST else shift if c < XCHUNKS else shift + ENTRIES + LANES) for c in range(CHUNKS + 1)]
+    return off, base, own_at, near_at
+
+
+def lanes(n):
+    return -(-n // LANES) * LANES
 
 
 def moe_kernel(sizes, ring, step, checked, sel_in, gate_in, x_hbm, up_hbm, down_hbm, y_ref, ok_ref,
                x_chip, out, rows_in, picked, acc, hot,
-               sel_row, sels, slots, toks_a, toks_b, sel_col, gate_col, need_col, pos_out, square, ok_mine, ok_other,
+               sel_row, sels, slots, toks_a, toks_b, toks_c, sel_col, gate_col, need_col, pos_out, square, ok_mine, ok_other,
                up_buf, down_buf,
                x_sem, up_sem, down_sem, send_sel, recv_sel, send_x, recv_x, send_link, recv_link, send_fwd, recv_fwd,
                send_near, recv_near, send_ok, recv_ok):
@@ -102,14 +116,6 @@
     high = mm(gather, mm((sel_in[...] >> 5).astype(F32), spread) * inside)
     low = mm(gather, mm((sel_in[...] & 31).astype(F32), spread) * inside)
     sel_row[...] = (high * 32.0 + low).astype(I32)
-    square[...] = jnp.zeros_like(square)
-    square[0:experts, 0:cap] = sel_in[...].astype(F32)
-    square[experts:2 * experts, 0:cap] = gate_in[...]
-    turned = square[...].T
-    for e in range(experts):
-        sel_col[e * cap:(e + 1) * cap, :] = turned[0:cap, e:e + 1].astype(I32)
-        gate_col[e * cap:(e + 1) * cap, :] = turned[0:cap, experts + e:experts + e + 1]
-
     pl.semaphore_wait(barrier, 4 if checked else 3)
     sel_send = [remote(sel_row, sels.at[me], send_sel.at[i], recv_sel.at[i], peer) for i, peer in enumerate(peers)]
     for copy in sel_send:
@@ -118,10 +124,17 @@
     to_near = remote(x_chip.at[own_rows], x_chip.at[own_rows], send_x, recv_x, near)
     to_near.start()
     sels[me] = sel_row[...]
+    square[...] = jnp.zeros_like(square)
+    square[0:experts, 0:cap] = sel_in[...].astype(F32)
+    square[experts:2 * experts, 0:cap] = gate_in[...]
+    turned = square[...].T
+    for e in range(experts):
+        sel_col[e * cap:(e + 1) * cap, :] = turned[0:cap, e:e + 1].astype(I32)
+        gate_col[e * cap:(e + 1) * cap, :] = turned[0:cap, experts + e:experts + e + 1]
 
     before = flag(iota((LANES, LANES), 0) < iota((LANES, LANES), 1))
     ones = jnp.ones((LANES, LANES), F32)
-    rows_before = flag(iota((GROUPS * 8, GROUPS * 8), 1) < iota((GROUPS * 8, GROUPS * 8), 0))
+    rows_before = flag(iota((XGROUPS * 8, XGROUPS * 8), 1) < iota((XGROUPS * 8, XGROUPS * 8), 0))
     for copy in sel_send:
         copy.wait_recv()
 
@@ -129,17 +142,22 @@
         start = (1 - c) * (2 * tok)
         seen = jnp.zeros((8, LANES), F32)
         firsts, fit = [], jnp.ones((1, 1), F32)
-        for j in range(GROUPS):
-            row = jnp.concatenate([sels[2 * c, j:j + 1, :], sels[2 * c + 1, j:j + 1, :]], axis=1) - start
+        lane = iota((1, 2 * LANES), 1) % LANES
+        for j in range(XGROUPS):
+            k = X_FROM[j] * cap // LANES
+            row = jnp.concatenate([sels[2 * c, k:k + 1, :], sels[2 * c + 1, k:k + 1, :]], axis=1) - start
+            if X_FROM[j + 1] - X_FROM[j] < per_group:
+                from_lane = (X_FROM[j] % per_group) * cap
+                row = jnp.where((lane >= from_lane) & (lane < from_lane + (X_FROM[j + 1] - X_FROM[j]) * cap), row, -1)
             row_high = flag(iota((8, 2 * LANES), 0) == (row >> 7))
             row_low = flag(iota((LANES, 2 * LANES), 0) == (row & 127))
             need = flag(mm_t(row_high, row_low) > 0.5)
             firsts.append(need * (1.0 - seen))
             seen = jnp.maximum(seen, need)
-            fit = fit * flag(total(seen) < 2.0 * off[j + 1] + 0.5)
+            fit = fit * flag(total(seen) < 2.0 * off[X_LAST[j] + 1] + 0.5)
         first = jnp.concatenate(firsts, axis=0)
         place = mm(first, before) + mm(rows_before, mm(first, ones))
-        pos = sum(firsts[j] * (place[8 * j:8 * j + 8] + 1.0) for j in range(GROUPS)) - 1.0
+        pos = sum(firsts[j] * (place[8 * j:8 * j + 8] + 1.0) for j in range(XGROUPS)) - 1.0
         return pos.astype(I32), total(seen), fit
 
     def entry_order(d, sent_rows):
@@ -152,13 +170,10 @@
         end = jnp.floor((sent_rows + 1.0) * 0.5)
         for j in range(GROUPS):
             row = slice(j, j + 1)
-            begin = jnp.maximum(end, float(off[j + 2]))
-            place = rank[row] + begin
-            end = begin + count[row]
-            if j == GROUPS - 1:
-                later = jnp.maximum(begin + count_early[row], float(off[CHUNKS - 1]))
-                place = jnp.where(lane[row] < LANES // 2, place, rank[row] - count_early[row] + later)
-                end = later + count[row] - count_early[row]
+            begin = jnp.maximum(end, float(off[FIRST + 2 * j]))
+            later = jnp.maximum(begin + count_early[row], float(off[FIRST + 2 * j + 1]))
+            place = rank[row] + jnp.where(lane[row] < LANES // 2, begin, later - count_early[row])
+            end = later + count[row] - count_early[row]
             slots[d, row, :] = (away[row] * (place + 1.0) - 1.0).astype(I32)
         return flag(end < off[CHUNKS] + 0.5)
 
@@ -184,13 +199,13 @@
         forward.append(remote(mine, theirs, send_fwd.at[c], recv_fwd.at[c], near))
     pass_near = []
     for j in range(GROUPS):
-        pass_near.append(remote(rows_in.at[pl.ds(own_at + j * LANES, LANES)], rows_in.at[pl.ds(near_at + j * LANES, LANES)],
+        pass_near.append(remote(rows_in.at[pl.ds(own_at + j * LANES, LANES)], rows_in.at[pl.ds(near_at[j], LANES)],
                                 send_near.at[j], recv_near.at[j], near))
 
-    pack(0, 2)
-    link[0].start()
-    link[1].start()
-    pack(2, 4)
+    pack(0, FIRST)
+    for c in range(FIRST):
+        link[c].start()
+    pack(FIRST, XCHUNKS)
 
     wanted, rows_got, fit_in = row_order(chip)
     fit = fit * fit_in
@@ -201,7 +216,7 @@
     slot = wanted >> 1
     side = jnp.where((wanted & 1) == core, 0, 1)
     where_in = jnp.full((8, LANES), -1, I32)
-    for c in range(GROUPS):
+    for c in range(XCHUNKS):
         here = (slot >= off[c]) & (slot < off[c + 1]) & (wanted >= 0)
         where_in = jnp.where(here, base[c] - off[c] + slot + side * sizes[c], where_in)
     where_in = where_in.astype(F32)
@@ -226,7 +241,7 @@
             row = sels[d, k:k + 1, :]
             values.append(jnp.where(at == 0, row >> 5, jnp.where(at == 1, row & 31, 1)).astype(F32))
     values = jnp.concatenate(values, axis=1)
-    for c in range(2, CHUNKS):
+    for c in range(FIRST, CHUNKS):
         size = sizes[c]
         at = iota((2 * size, LANES), 0)
         for f, d in enumerate((far, diag)):
@@ -236,27 +251,42 @@
                 hot[0:2 * size, block:block + LANES] = flag(key == slots[d, k:k + 1, :]).astype(BF16)
         sums = mm_t(values, hot[0:2 * size, 0:2 * ENTRIES])
         token = jnp.where(sums[2:3] > 0.5, sums[0:1] * 32.0 + sums[1:2], -1.0).astype(I32)
-        if c < 5:
-            toks_a[:, base[c] - base[2]:base[c + 1] - base[2]] = token
-        else:
-            toks_b[:, base[c] - base[5]:base[c + 1] - base[5]] = token
+        toks, start = (toks_a, FIRST) if c < XCHUNKS else (toks_b, XCHUNKS) if c < LATE else (toks_c, LATE)
+        at = base[c] - base[start]
+        toks[:, at:at + 2 * size] = token
 
     if checked:
         ok_mine[...] = jnp.broadcast_to(fit, ok_mine.shape)
         ok_send = remote(ok_mine, ok_other, send_ok, recv_ok, other_group, "dp")
         ok_send.start()
 
-    def arrive(c):
+    def pass_on(c):
         link[c].wait_recv()
         forward[c].start()
-        r0, size = c * LANES, 2 * sizes[c]
-        hot[r0:ENTRIES, 0:size] = flag(need_col[r0:, :] == iota((ENTRIES - r0, size), 1) + base[c]).astype(BF16)
-        forward[c].wait_recv()
+
+    def arrive(j):
+        r0, lo, hi = X_FROM[j] * cap, (X_LAST[j - 1] + 1 if j else 0), X_LAST[j] + 1
+        size = base[hi - 1] + 2 * sizes[hi - 1] - base[lo]
+        if j < 2:
+            pass_on(lo)
+        hot[r0:ENTRIES, 0:size] = flag(need_col[r0:, :] == iota((ENTRIES - r0, size), 1) + base[lo]).astype(BF16)
+        for c in range(lo, hi):
+            forward[c].wait_recv()
 
         def write(cols):
             picked[r0:, cols] = picked[r0:, cols] + jnp.dot(
-                hot[r0:ENTRIES, 0:size], rows_in[base[c]:base[c] + size, cols], preferred_element_type=F32).astype(BF16)
+                hot[r0:ENTRIES, 0:size], rows_in[base[lo]:base[lo] + size, cols], preferred_element_type=F32).astype(BF16)
         by_columns(write)
+
+    def own_hot(at, d, k):
+        hot[0:tok, at:at + LANES] = flag(iota((tok, LANES), 0) + me * tok == sels[d, k:k + 1, :]).astype(BF16)
+
+    def toks_hot(at, toks):
+        size = toks.shape[1]
+        hot[0:tok, at:at + size] = flag(iota((tok, size), 0) + me * tok == toks[...]).astype(BF16)
+
+    def rows_of(at, row, size, cols):
+        return jnp.dot(hot[0:tok, at:at + size], rows_in[row:row + size, cols], preferred_element_type=F32)
 
     def give(c):
         size = sizes[c]
@@ -269,15 +299,20 @@
         def write(cols):
             packed = jnp.dot(hot[0:size, 0:depth], rows_in[own_at:own_at + depth, cols],
                              preferred_element_type=F32).astype(BF16)
-            if c < GROUPS:
+            if c < XCHUNKS:
                 packed = packed + out[off[c]:off[c + 1], cols]
             out[off[c]:off[c + 1], cols] = packed
         by_columns(write)
         link[c].start()
 
     def expert(e, carry):
-        for c in range(GROUPS):
-            pl.when(e == c * per_group)(functools.partial(arrive, c))
+        for j in range(XGROUPS):
+            pl.when(e == X_FROM[j])(functools.partial(arrive, j))
+        for j in range(2, XGROUPS):
+            for c in range(X_LAST[j - 1] + 1, X_LAST[j] + 1):
+                pl.when(e == X_FROM[j] - 1)(functools.partial(pass_on, c))
+        for c in range(XCHUNKS, LATE - 1):
+            pl.when(e == SENT_AFTER[c] + 6)(functools.partial(pass_on, c))
         rows = pl.ds(pl.multiple_of(e * cap, cap), cap)
         own = pl.ds(pl.multiple_of(own_at + e * cap, 32), cap)
         up_copy(e).wait()
@@ -298,7 +333,7 @@
         def _():
             down_copy(e + ring).start()
 
-        for c in range(2, CHUNKS):
+        for c in range(FIRST, CHUNKS):
             pl.when(e == SENT_AFTER[c])(functools.partial(give, c))
         for j in range(GROUPS):
             pl.when(e == j * per_group + per_group - 1)(pass_near[j].start)
@@ -306,35 +341,29 @@
 
     lax.fori_loop(0, experts, expert, 0)
 
-    link[4].wait_recv()
-    forward[4].start()
-    early = base[5] - own_at
-    for at, d in ((0, me), (ENTRIES, near)):
-        for k in range(GROUPS):
-            hot[0:tok, at + k * LANES:at + (k + 1) * LANES] = flag(
-                iota((tok, LANES), 0) + me * tok == sels[d, k:k + 1, :]).astype(BF16)
-    hot[0:tok, 2 * ENTRIES:early] = flag(iota((tok, early - 2 * ENTRIES), 0) + me * tok == toks_a[...]).astype(BF16)
-    for copy in pass_near:
+    pass_on(LATE - 1)
+    start = near_at[0]
+    for k in range(GROUPS):
+        own_hot(near_at[k] - start, near, k)
+        own_hot(own_at + k * LANES - start, me, k)
+    toks_hot(base[FIRST] - start, toks_a)
+    toks_hot(base[XCHUNKS] - start, toks_b)
+    for copy in pass_near + forward[XCHUNKS:LATE]:
         copy.wait_recv()
-    forward[4].wait_recv()
 
     def add_early(cols):
-        acc[:, cols] = x_chip[own_rows, cols].astype(F32) + jnp.dot(
-            hot[0:tok, 0:early], rows_in[own_at:base[5], cols], preferred_element_type=F32)
+        acc[:, cols] = x_chip[own_rows, cols].astype(F32) + rows_of(0, start, base[LATE] - start, cols)
     by_columns(add_early)
 
-    late = base[CHUNKS] - base[5]
-    for c in (5, 6):
-        link[c].wait_recv()
-        forward[c].start()
-    hot[0:tok, 0:late] = flag(iota((tok, late), 0) + me * tok == toks_b[...]).astype(BF16)
-    for c in (5, 6):
+    for c in range(LATE, CHUNKS):
+        pass_on(c)
+    toks_hot(0, toks_c)
+    for c in range(LATE, CHUNKS):
         forward[c].wait_recv()
 
-    def add_late(cols):
-        y_ref[:, cols] = (acc[:, cols] + jnp.dot(hot[0:tok, 0:late], rows_in[base[5]:base[CHUNKS], cols],
-                                                 preferred_element_type=F32)).astype(BF16)
-    by_columns(add_late)
+    def add_last(cols):
+        y_ref[:, cols] = (acc[:, cols] + rows_of(0, base[LATE], base[CHUNKS] - base[LATE], cols)).astype(BF16)
+    by_columns(add_last)
 
     if checked:
         ok_send.wait()
@@ -350,7 +379,7 @@
     def layer(sizes, ring, step, checked, collective_id, sel, gate, x_loc, up_loc, down_loc):
         tok, width = x_loc.shape
         experts, _, hidden = up_loc.shape
-        off, base, own_at, _ = plan(sizes)
+        off, base, own_at, near_at = plan(sizes)
         vmem = pl.BlockSpec(memory_space=pltpu.VMEM)
         hbm = pl.BlockSpec(memory_space=pl.ANY)
         dma = pltpu.SemaphoreType.DMA
@@ -366,12 +395,13 @@
                 pltpu.VMEM((base[CHUNKS], width), BF16),
                 pltpu.VMEM((ENTRIES, width), BF16),
                 pltpu.VMEM((tok, width), F32),
-                pltpu.VMEM((tok, max(2 * tok, base[5] - own_at)), BF16),
+                pltpu.VMEM((tok, max(2 * tok, lanes(base[LATE] - near_at[0]))), BF16),
                 pltpu.VMEM((GROUPS, LANES), I32),
                 pltpu.VMEM((4, GROUPS, LANES), I32),
                 pltpu.VMEM((4, GROUPS, LANES), I32),
-                pltpu.VMEM((1, base[5] - base[2]), I32),
-                pltpu.VMEM((1, base[CHUNKS] - base[5]), I32),
+                pltpu.VMEM((1, 2 * (off[XCHUNKS] - off[FIRST])), I32),
+                pltpu.VMEM((1, 2 * (off[LATE] - off[XCHUNKS])), I32),
+                pltpu.VMEM((1, 2 * (off[CHUNKS] - off[LATE])), I32),
                 pltpu.VMEM((ENTRIES, 1), I32),
                 pltpu.VMEM((ENTRIES, 1), F32),
                 pltpu.VMEM((ENTRIES, 1), I32),
@@ -385,7 +415,7 @@
                 each, each, each, each, dma((GROUPS,)), dma((GROUPS,)), dma, dma,
             ],
             compiler_params=pltpu.CompilerParams(collective_id=collective_id, has_side_effects=True,
-                                                 vmem_limit_bytes=64 * 1024 * 1024 - 65536),
+                                                 vmem_limit_bytes=56 * 1024 * 1024),
         )(sel, gate, x_loc, up_loc, down_loc)
 
     def local_layer(x_loc, sel_loc, gate_loc, up_loc, down_loc):

time: 79.1 us -> 67.4 us (0.85)
  Pallas kernels: 75.1 us -> 64.9 us
  local copies, waits for them, and re-layouts: 3.16 us -> 1.33 us
    pallas_call x1, Pallas kernels: 75.1 us -> 64.9 us  [layer(): pl.pallas_call(functools.partial(moe_kernel, sizes, ring, step, checked),...]
    unnamed x1 -> x7, local copies, waits for them, and re-layouts: 3.16 us -> 1.33 us
where the time goes in v5:
time: 67.4 us; the launch traced here: 67 us
  Pallas kernels  64.9 us (96%)
  local copies, waits for them, and re-layouts  1.33 us (2%)
  between operations  0.73 us (1%)
    pallas_call x1, Pallas kernels, layer(): pl.pallas_call(functools.partial(moe_kernel, sizes, ring, step, checked),...  64.9 us

profile of v5, /device:TPU:0, one launch (start us, length us, event | category | flops | bytes accessed | tf_op | source)
XLA Modules:
  0.0 67.0 jit_solution(6597755387379226859)
XLA Ops:
  0.0 0.0 copy-start
  0.0 0.0 copy-start.1
  0.0 0.0 copy-start.2
  0.0 64.9 %shard_map.57 = (bf16[512,2048]{1,0:T(8,128)(2,1)S(1)}, f32[1,1]{1,0:T(1,128)}) custom-call(s32[16,32]{1,0:T(8,128)} %sel_in.1, f32[16,32]{1,0:T(8,128)} %gate_in.1, bf16[512,2048]{1,0:T(8,128)(2,1)} %x_hbm.1, bf16[16,2048,1024]{2,1,0:T(8,128)(2,1)} %up_hbm.1, bf16[16,1024,2048]{2,1,0:T(8,128)(2,1)} %down_hbm.1), custom_call_target="tpu_custom_call" | custom-call | tf_op jit(solution)/shard_map/pallas_call | solution.py:387
  65.6 0.0 copy-done
  65.6 0.0 copy-done.1
  65.7 0.0 copy-done.2
  65.7 1.3 %copy.11 = bf16[512,2048]{1,0:T(8,128)(2,1)} copy(bf16[512,2048]{1,0:T(8,128)(2,1)S(1)} %get-tuple-element.29) | data formatting | bytes 4194304
  (1 shorter events, 0.0 us)
Async XLA Ops:
  0.0 65.6 %copy-start = (bf16[512,2048]{1,0:T(8,128)(2,1)S(1)}, bf16[512,2048]{1,0:T(8,128)(2,1)}, u32[]{:S(2)}) copy-start(bf16[512,2048]{1,0:T(8,128)(2,1)} %x_hbm.1) | copy-start | bytes 6291460
  0.0 65.6 %copy-start.1 = (s32[16,32]{1,0:T(8,128)S(1)}, s32[16,32]{1,0:T(8,128)}, u32[]{:S(2)}) copy-start(s32[16,32]{1,0:T(8,128)} %sel_in.1) | copy-start | bytes 6148
  0.0 65.7 %copy-start.2 = (f32[16,32]{1,0:T(8,128)S(1)}, f32[16,32]{1,0:T(8,128)}, u32[]{:S(2)}) copy-start(f32[16,32]{1,0:T(8,128)} %gate_in.1) | copy-start | bytes 6148

commit v6 on v5

--- a/solution.py
+++ b/solution.py
@@ -22,7 +22,7 @@
 XGROUPS = len(X_LAST)
 XCHUNKS = X_LAST[-1] + 1
 LATE = CHUNKS - 2
-FIT = dict(sizes=(64, 48, 32, 32, 48, 32, 48, 48, 48, 48, 64, 64), ring=3, step=2048, checked=True)
+FIT = dict(sizes=(64, 48, 32, 32, 48, 32, 48, 48, 48, 48, 64, 64), ring=4, step=2048, checked=True)
 FULL = dict(sizes=(64, 64, 64, 64, 128, 64, 64, 192, 128, 64, 64, 64), ring=2, step=512, checked=False)
 
 
@@ -89,11 +89,11 @@
         return pltpu.make_async_remote_copy(src_ref=src, dst_ref=dst, send_sem=send, recv_sem=recv,
                                             device_id={axis: peer}, device_id_type=MESH)
 
-    def by_columns(write):
+    def by_columns(write, start=0, stop=width):
         if step == width:
-            write(slice(None))
+            write(slice(start, stop))
         else:
-            @pl.loop(0, width // step)
+            @pl.loop(start // step, stop // step)
             def _(n):
                 write(pl.ds(pl.multiple_of(n * step, step), step))
 
@@ -121,8 +121,12 @@
     for copy in sel_send:
         copy.start()
     load_x.wait()
-    to_near = remote(x_chip.at[own_rows], x_chip.at[own_rows], send_x, recv_x, near)
-    to_near.start()
+    halves = [slice(h * width // 2, (h + 1) * width // 2) for h in range(2)]
+    to_near = []
+    for h, cols in enumerate(halves):
+        block = x_chip.at[own_rows, pl.ds(cols.start, width // 2)]
+        to_near.append(remote(block, block, send_x.at[h], recv_x.at[h], near))
+        to_near[h].start()
     sels[me] = sel_row[...]
     square[...] = jnp.zeros_like(square)
     square[0:experts, 0:cap] = sel_in[...].astype(F32)
@@ -179,33 +183,49 @@
 
     pos, rows_sent, fit = row_order(1 - chip)
     pos_out[...] = jnp.where((pos & 1) == core, pos >> 1, -1)
-    to_near.wait_recv()
-
-    def pack(lo, hi):
+
+    def pack_hot(lo, hi):
         size = off[hi] - off[lo]
         for b in range(8):
             hot[0:size, b * LANES:(b + 1) * LANES] = flag(iota((size, LANES), 0) + off[lo] == pos_out[b:b + 1, :]).astype(BF16)
 
+    def pack(skip, lo, hi, start=0, stop=width):
+        size = off[hi] - off[lo]
+
         def write(cols):
-            out[off[lo]:off[hi], cols] = jnp.dot(hot[0:size, 0:2 * tok], x_chip[:, cols],
+            out[off[lo]:off[hi], cols] = jnp.dot(hot[skip:skip + size, 0:2 * tok], x_chip[:, cols],
                                                  preferred_element_type=F32).astype(BF16)
-        by_columns(write)
-
-    link, forward = [], []
+        by_columns(write, start, stop)
+
+    link, link0, forward = [], [], []
     for c in range(CHUNKS):
         mine = rows_in.at[pl.ds(base[c], sizes[c])]
         theirs = rows_in.at[pl.ds(base[c] + sizes[c], sizes[c])]
-        link.append(remote(out.at[pl.ds(off[c], sizes[c])], mine, send_link.at[c], recv_link.at[c], far))
+        if c == 0:
+            for h, cols in enumerate(halves):
+                part = pl.ds(cols.start, width // 2)
+                link0.append(remote(out.at[pl.ds(0, sizes[0]), part], rows_in.at[pl.ds(base[0], sizes[0]), part],
+                                    send_link.at[h * CHUNKS], recv_link.at[h * CHUNKS], far))
+        link.append(link0 if c == 0 else [
+            remote(out.at[pl.ds(off[c], sizes[c])], mine, send_link.at[c], recv_link.at[c], far)])
         forward.append(remote(mine, theirs, send_fwd.at[c], recv_fwd.at[c], near))
     pass_near = []
     for j in range(GROUPS):
         pass_near.append(remote(rows_in.at[pl.ds(own_at + j * LANES, LANES)], rows_in.at[pl.ds(near_at[j], LANES)],
                                 send_near.at[j], recv_near.at[j], near))
 
-    pack(0, FIRST)
-    for c in range(FIRST):
-        link[c].start()
-    pack(FIRST, XCHUNKS)
+    pack_hot(0, FIRST)
+    to_near[0].wait_recv()
+    pack(0, 0, 1, halves[0].start, halves[0].stop)
+    link0[0].start()
+    to_near[1].wait_recv()
+    pack(0, 0, 1, halves[1].start, halves[1].stop)
+    link0[1].start()
+    pack(off[1], 1, FIRST)
+    for c in range(1, FIRST):
+        link[c][0].start()
+    pack_hot(FIRST, XCHUNKS)
+    pack(0, FIRST, XCHUNKS)
 
     wanted, rows_got, fit_in = row_order(chip)
     fit = fit * fit_in
@@ -261,7 +281,8 @@
         ok_send.start()
 
     def pass_on(c):
-        link[c].wait_recv()
+        for copy in link[c]:
+            copy.wait_recv()
         forward[c].start()
 
     def arrive(j):
@@ -303,7 +324,7 @@
                 packed = packed + out[off[c]:off[c + 1], cols]
             out[off[c]:off[c + 1], cols] = packed
         by_columns(write)
-        link[c].start()
+        link[c][0].start()
 
     def expert(e, carry):
         for j in range(XGROUPS):
@@ -370,8 +391,7 @@
         ok_ref[0, 0] = jnp.min(ok_mine[...] * ok_other[...])
     else:
         ok_ref[0, 0] = 1.0
-    to_near.wait_send()
-    for copy in sel_send + link + forward + pass_near:
+    for copy in to_near + sel_send + sum(link, []) + forward + pass_near:
         copy.wait_send()
 
 
@@ -411,11 +431,11 @@
                 pltpu.VMEM((8, LANES), F32),
                 pltpu.VMEM((ring, width, hidden), BF16),
                 pltpu.VMEM((ring, hidden, width), BF16),
-                dma, dma((ring,)), dma((ring,)), dma((3,)), dma((3,)), dma, dma,
-                each, each, each, each, dma((GROUPS,)), dma((GROUPS,)), dma, dma,
+                dma, dma((ring,)), dma((ring,)), dma((3,)), dma((3,)), dma((2,)), dma((2,)),
+                dma((CHUNKS + 1,)), dma((CHUNKS + 1,)), each, each, dma((GROUPS,)), dma((GROUPS,)), dma, dma,
             ],
             compiler_params=pltpu.CompilerParams(collective_id=collective_id, has_side_effects=True,
-                                                 vmem_limit_bytes=56 * 1024 * 1024),
+                                                 vmem_limit_bytes=58 * 1024 * 1024),
         )(sel, gate, x_loc, up_loc, down_loc)
 
     def local_layer(x_loc, sel_loc, gate_loc, up_loc, down_loc):

time: 67.4 us -> 66.5 us (0.987)
  Pallas kernels: 64.9 us -> 63.9 us
    pallas_call x1, Pallas kernels: 64.9 us -> 63.9 us  [layer(): pl.pallas_call(functools.partial(moe_kernel, sizes, ring, step, checked),...]
where the time goes in v6:
time: 66.5 us; the launch traced here: 65.9 us
  Pallas kernels  63.9 us (96%)
  local copies, waits for them, and re-layouts  1.33 us (2%)
  between operations  0.73 us (1%)
    pallas_call x1, Pallas kernels, layer(): pl.pallas_call(functools.partial(moe_kernel, sizes, ring, step, checked),...  63.9 us
    unnamed x7, local copies, waits for them, and re-layouts  1.33 us

profile of v6, /device:TPU:0, one launch (start us, length us, event | category | flops | bytes accessed | tf_op | source)
XLA Modules:
  0.0 65.9 jit_solution(3992491669906422512)
XLA Ops:
  0.0 0.0 copy-start
  0.0 0.0 copy-start.1
  0.0 0.0 copy-start.2
  0.0 63.9 %shard_map.57 = (bf16[512,2048]{1,0:T(8,128)(2,1)S(1)}, f32[1,1]{1,0:T(1,128)}) custom-call(s32[16,32]{1,0:T(8,128)} %sel_in.1, f32[16,32]{1,0:T(8,128)} %gate_in.1, bf16[512,2048]{1,0:T(8,128)(2,1)} %x_hbm.1, bf16[16,2048,1024]{2,1,0:T(8,128)(2,1)} %up_hbm.1, bf16[16,1024,2048]{2,1,0:T(8,128)(2,1)} %down_hbm.1), custom_call_target="tpu_custom_call" | custom-call | tf_op jit(solution)/shard_map/pallas_call | solution.py:407
  64.6 0.0 copy-done
  64.6 0.0 copy-done.1
  64.6 0.0 copy-done.2
  64.6 1.3 %copy.11 = bf16[512,2048]{1,0:T(8,128)(2,1)} copy(bf16[512,2048]{1,0:T(8,128)(2,1)S(1)} %get-tuple-element.29) | data formatting | bytes 4194304
  (1 shorter events, 0.0 us)
Async XLA Ops:
  0.0 64.6 %copy-start = (bf16[512,2048]{1,0:T(8,128)(2,1)S(1)}, bf16[512,2048]{1,0:T(8,128)(2,1)}, u32[]{:S(2)}) copy-start(bf16[512,2048]{1,0:T(8,128)(2,1)} %x_hbm.1) | copy-start | bytes 6291460
  0.0 64.6 %copy-start.1 = (s32[16,32]{1,0:T(8,128)S(1)}, s32[16,32]{1,0:T(8,128)}, u32[]{:S(2)}) copy-start(s32[16,32]{1,0:T(8,128)} %sel_in.1) | copy-start | bytes 6148
  0.0 64.6 %copy-start.2 = (f32[16,32]{1,0:T(8,128)S(1)}, f32[16,32]{1,0:T(8,128)}, u32[]{:S(2)}) copy-start(f32[16,32]{1,0:T(8,128)} %gate_in.1) | copy-start | bytes 6148

commit v7 on v6

--- a/solution.py
+++ b/solution.py
@@ -14,16 +14,16 @@
 BF16 = jnp.bfloat16
 F32 = jnp.float32
 I32 = jnp.int32
-SENT_AFTER = (None, None, None, None, 1, 3, 5, 7, 9, 11, 13, 15)
+SENT_AFTER = (None, None, None, 1, 3, 5, 7, 9, 11, 13, 14, 15)
 CHUNKS = len(SENT_AFTER)
-FIRST = 4
+FIRST = 3
 X_FROM = (0, 2, 4, 6, 8, 12, 16)
-X_LAST = (0, 1, 2, 3, 4, 6)
+X_LAST = (0, 1, 2, 3, 4, 5)
 XGROUPS = len(X_LAST)
 XCHUNKS = X_LAST[-1] + 1
-LATE = CHUNKS - 2
-FIT = dict(sizes=(64, 48, 32, 32, 48, 32, 48, 48, 48, 48, 64, 64), ring=4, step=2048, checked=True)
-FULL = dict(sizes=(64, 64, 64, 64, 128, 64, 64, 192, 128, 64, 64, 64), ring=2, step=512, checked=False)
+LATE = CHUNKS - 3
+FIT = dict(sizes=(64, 48, 32, 48, 32, 48, 48, 48, 48, 48, 32, 48), ring=4, step=2048, checked=True)
+FULL = dict(sizes=(64, 64, 64, 64, 128, 128, 192, 128, 64, 64, 32, 32), ring=2, step=512, checked=False)
 
 
 def iota(shape, dim):
@@ -167,18 +167,23 @@
     def entry_order(d, sent_rows):
         away = flag((sels[d] >> 10) != d // 2)
         rank = mm(away, before)
-        lane = iota((GROUPS, LANES), 1)
-        early = flag(lane < LANES // 2)
-        count = jnp.sum(away, axis=1, keepdims=True)
-        count_early = jnp.sum(away * early, axis=1, keepdims=True)
+        lane = iota((1, LANES), 1)
         end = jnp.floor((sent_rows + 1.0) * 0.5)
-        for j in range(GROUPS):
-            row = slice(j, j + 1)
-            begin = jnp.maximum(end, float(off[FIRST + 2 * j]))
-            later = jnp.maximum(begin + count_early[row], float(off[FIRST + 2 * j + 1]))
-            place = rank[row] + jnp.where(lane[row] < LANES // 2, begin, later - count_early[row])
-            end = later + count[row] - count_early[row]
-            slots[d, row, :] = (away[row] * (place + 1.0) - 1.0).astype(I32)
+        stop = 0
+        for c in range(FIRST, CHUNKS):
+            start, stop = stop, (SENT_AFTER[c] + 1) * cap
+            row = slice(start // LANES, start // LANES + 1)
+            lo, hi = start % LANES, start % LANES + stop - start
+            if lo == 0:
+                earlier, place = jnp.zeros((1, 1), F32), jnp.zeros((1, LANES), F32)
+            here = (lane >= lo) & (lane < hi)
+            count = jnp.sum(jnp.where(here, away[row], 0.0), axis=1, keepdims=True)
+            begin = jnp.maximum(end, float(off[c]))
+            place = jnp.where(here, rank[row] - earlier + begin, place)
+            earlier = earlier + count
+            end = begin + count
+            if hi == LANES:
+                slots[d, row, :] = (away[row] * (place + 1.0) - 1.0).astype(I32)
         return flag(end < off[CHUNKS] + 0.5)
 
     pos, rows_sent, fit = row_order(1 - chip)
@@ -337,6 +342,7 @@
         rows = pl.ds(pl.multiple_of(e * cap, cap), cap)
         own = pl.ds(pl.multiple_of(own_at + e * cap, 32), cap)
         up_copy(e).wait()
+        down_copy(e).wait()
         z = jnp.dot(picked[rows, :], up_buf[e % ring], preferred_element_type=F32)
         act = (0.5 * z * (1.0 + jnp.tanh(0.7978845608028654 * (z + 0.044715 * (z * z * z))))).astype(BF16)
 
@@ -344,7 +350,6 @@
         def _():
             up_copy(e + ring).start()
 
-        down_copy(e).wait()
         for n in range(width // 512):
             cols = slice(n * 512, (n + 1) * 512)
             o = jnp.dot(act, down_buf[e % ring, :, cols], preferred_element_type=F32)

time: 66.5 us -> 65.6 us (0.986)
  Pallas kernels: 63.9 us -> 63.2 us
    pallas_call x1, Pallas kernels: 63.9 us -> 63.2 us  [layer(): pl.pallas_call(functools.partial(moe_kernel, sizes, ring, step, checked),...]
where the time goes in v7:
time: 65.6 us; the launch traced here: 65.2 us
  Pallas kernels  63.2 us (96%)
  local copies, waits for them, and re-layouts  1.33 us (2%)
  between operations  0.73 us (1%)
    pallas_call x1, Pallas kernels, layer(): pl.pallas_call(functools.partial(moe_kernel, sizes, ring, step, checked),...  63.2 us
    unnamed x7, local copies, waits for them, and re-layouts  1.33 us

profile of v7, /device:TPU:0, one launch (start us, length us, event | category | flops | bytes accessed | tf_op | source)
XLA Modules:
  0.0 65.2 jit_solution(15001625930592856457)
XLA Ops:
  0.0 0.0 copy-start
  0.0 0.0 copy-start.1
  0.0 0.0 copy-start.2
  0.0 63.2 %shard_map.57 = (bf16[512,2048]{1,0:T(8,128)(2,1)S(1)}, f32[1,1]{1,0:T(1,128)}) custom-call(s32[16,32]{1,0:T(8,128)} %sel_in.1, f32[16,32]{1,0:T(8,128)} %gate_in.1, bf16[512,2048]{1,0:T(8,128)(2,1)} %x_hbm.1, bf16[16,2048,1024]{2,1,0:T(8,128)(2,1)} %up_hbm.1, bf16[16,1024,2048]{2,1,0:T(8,128)(2,1)} %down_hbm.1), custom_call_target="tpu_custom_call" | custom-call | tf_op jit(solution)/shard_map/pallas_call | solution.py:412
  63.9 0.0 copy-done
  63.9 0.0 copy-done.1
  63.9 0.0 copy-done.2
  63.9 1.3 %copy.11 = bf16[512,2048]{1,0:T(8,128)(2,1)} copy(bf16[512,2048]{1,0:T(8,128)(2,1)S(1)} %get-tuple-element.29) | data formatting | bytes 4194304
  (1 shorter events, 0.0 us)
Async XLA Ops:
  0.0 63.9 %copy-start = (bf16[512,2048]{1,0:T(8,128)(2,1)S(1)}, bf16[512,2048]{1,0:T(8,128)(2,1)}, u32[]{:S(2)}) copy-start(bf16[512,2048]{1,0:T(8,128)(2,1)} %x_hbm.1) | copy-start | bytes 6291460
  0.0 63.9 %copy-start.1 = (s32[16,32]{1,0:T(8,128)S(1)}, s32[16,32]{1,0:T(8,128)}, u32[]{:S(2)}) copy-start(s32[16,32]{1,0:T(8,128)} %sel_in.1) | copy-start | bytes 6148
  0.0 63.9 %copy-start.2 = (f32[16,32]{1,0:T(8,128)S(1)}, f32[16,32]{1,0:T(8,128)}, u32[]{:S(2)}) copy-start(f32[16,32]{1,0:T(8,128)} %gate_in.1) | copy-start | bytes 6148

commit v8 on v7

--- a/solution.py
+++ b/solution.py
@@ -259,26 +259,29 @@
         picked[:, cols] = jnp.dot(hot[0:ENTRIES, 0:2 * tok], x_chip[:, cols], preferred_element_type=F32).astype(BF16)
     by_columns(pick_local)
 
-    values = []
-    for d in (far, diag):
-        for k in range(GROUPS):
-            at = iota((8, LANES), 0)
-            row = sels[d, k:k + 1, :]
-            values.append(jnp.where(at == 0, row >> 5, jnp.where(at == 1, row & 31, 1)).astype(F32))
-    values = jnp.concatenate(values, axis=1)
-    for c in range(FIRST, CHUNKS):
-        size = sizes[c]
-        at = iota((2 * size, LANES), 0)
-        for f, d in enumerate((far, diag)):
-            key = jnp.where((at >= f * size) & (at < (f + 1) * size), at - f * size + off[c], -2)
+    def tokens(first, last):
+        values = []
+        for d in (far, diag):
             for k in range(GROUPS):
-                block = (f * GROUPS + k) * LANES
-                hot[0:2 * size, block:block + LANES] = flag(key == slots[d, k:k + 1, :]).astype(BF16)
-        sums = mm_t(values, hot[0:2 * size, 0:2 * ENTRIES])
-        token = jnp.where(sums[2:3] > 0.5, sums[0:1] * 32.0 + sums[1:2], -1.0).astype(I32)
-        toks, start = (toks_a, FIRST) if c < XCHUNKS else (toks_b, XCHUNKS) if c < LATE else (toks_c, LATE)
-        at = base[c] - base[start]
-        toks[:, at:at + 2 * size] = token
+                at = iota((8, LANES), 0)
+                row = sels[d, k:k + 1, :]
+                values.append(jnp.where(at == 0, row >> 5, jnp.where(at == 1, row & 31, 1)).astype(F32))
+        values = jnp.concatenate(values, axis=1)
+        for c in range(first, last):
+            size = sizes[c]
+            at = iota((2 * size, LANES), 0)
+            for f, d in enumerate((far, diag)):
+                key = jnp.where((at >= f * size) & (at < (f + 1) * size), at - f * size + off[c], -2)
+                for k in range(GROUPS):
+                    block = (f * GROUPS + k) * LANES
+                    hot[0:2 * size, block:block + LANES] = flag(key == slots[d, k:k + 1, :]).astype(BF16)
+            sums = mm_t(values, hot[0:2 * size, 0:2 * ENTRIES])
+            token = jnp.where(sums[2:3] > 0.5, sums[0:1] * 32.0 + sums[1:2], -1.0).astype(I32)
+            toks, start = (toks_a, FIRST) if c < XCHUNKS else (toks_b, XCHUNKS) if c < LATE else (toks_c, LATE)
+            at = base[c] - base[start]
+            toks[:, at:at + 2 * size] = token
+
+    tokens(FIRST, LATE)
 
     if checked:
         ok_mine[...] = jnp.broadcast_to(fit, ok_mine.shape)
@@ -295,6 +298,8 @@
         size = base[hi - 1] + 2 * sizes[hi - 1] - base[lo]
         if j < 2:
             pass_on(lo)
+        if j == 0:
+            tokens(LATE, CHUNKS)
         hot[r0:ENTRIES, 0:size] = flag(need_col[r0:, :] == iota((ENTRIES - r0, size), 1) + base[lo]).astype(BF16)
         for c in range(lo, hi):
             forward[c].wait_recv()

time: 65.6 us -> 65.8 us (level)
  no operation moved by 1% of the time
where the time goes in v8:
time: 65.8 us; the launch traced here: 65.4 us
  Pallas kernels  63.3 us (96%)
  local copies, waits for them, and re-layouts  1.33 us (2%)
  between operations  0.73 us (1%)
    pallas_call x1, Pallas kernels, layer(): pl.pallas_call(functools.partial(moe_kernel, sizes, ring, step, checked),...  63.3 us
    unnamed x7, local copies, waits for them, and re-layouts  1.33 us

profile of v8, /device:TPU:0, one launch (start us, length us, event | category | flops | bytes accessed | tf_op | source)
XLA Modules:
  0.0 65.4 jit_solution(13372054644353842149)
XLA Ops:
  0.0 0.0 copy-start
  0.0 0.0 copy-start.1
  0.0 0.0 copy-start.2
  0.0 63.3 %shard_map.57 = (bf16[512,2048]{1,0:T(8,128)(2,1)S(1)}, f32[1,1]{1,0:T(1,128)}) custom-call(s32[16,32]{1,0:T(8,128)} %sel_in.1, f32[16,32]{1,0:T(8,128)} %gate_in.1, bf16[512,2048]{1,0:T(8,128)(2,1)} %x_hbm.1, bf16[16,2048,1024]{2,1,0:T(8,128)(2,1)} %up_hbm.1, bf16[16,1024,2048]{2,1,0:T(8,128)(2,1)} %down_hbm.1), custom_call_target="tpu_custom_call" | custom-call | tf_op jit(solution)/shard_map/pallas_call | solution.py:417
  64.0 0.0 copy-done
  64.0 0.0 copy-done.1
  64.0 0.0 copy-done.2
  64.1 1.3 %copy.11 = bf16[512,2048]{1,0:T(8,128)(2,1)} copy(bf16[512,2048]{1,0:T(8,128)(2,1)S(1)} %get-tuple-element.29) | data formatting | bytes 4194304
  (1 shorter events, 0.0 us)
Async XLA Ops:
  0.0 64.0 %copy-start = (bf16[512,2048]{1,0:T(8,128)(2,1)S(1)}, bf16[512,2048]{1,0:T(8,128)(2,1)}, u32[]{:S(2)}) copy-start(bf16[512,2048]{1,0:T(8,128)(2,1)} %x_hbm.1) | copy-start | bytes 6291460
  0.0 64.0 %copy-start.1 = (s32[16,32]{1,0:T(8,128)S(1)}, s32[16,32]{1,0:T(8,128)}, u32[]{:S(2)}) copy-start(s32[16,32]{1,0:T(8,128)} %sel_in.1) | copy-start | bytes 6148
  0.0 64.0 %copy-start.2 = (f32[16,32]{1,0:T(8,128)S(1)}, f32[16,32]{1,0:T(8,128)}, u32[]{:S(2)}) copy-start(f32[16,32]{1,0:T(8,128)} %gate_in.1) | copy-start | bytes 6148
